TPU v7x, 32 devices: a whole 2x2x4 slice. The times are simulated.
32 devices in a mesh: lat: 4 (over z), lon: 8 (over y, x, core).
Axes of the slice: x: 2, y: 2, z: 4, core: 2. Of those that a mesh axis runs over, the one named last changes fastest.
Arguments:
- increments: bfloat16 [65536, 3, 128], P(('lat', 'lon')), may hold values from -6 to 6
- cotangent: bfloat16 [65536, 128], P(('lat', 'lon')), may hold values from -6 to 6
- owner_perm: int32 [32, 2048], P(('lat', 'lon')), may hold values from 0 to 2047, each once within a row
- coarse_index: int32 [2, 32768], P(None, ('lat', 'lon')), may hold values from 0 to 2047
- coarse_weight: float32 [32768], P(('lat', 'lon')), may hold values from 0.2 to 0.8
- back_index: int32 [2, 65536], P(None, ('lat', 'lon')), may hold values from 0 to 1023
- back_weight: float32 [65536], P(('lat', 'lon')), may hold values from 0.2 to 0.8
- lw_scale: float32 [16, 32768], P(None, ('lat', 'lon')), may hold values from 0.1 to 1
- sw_scale: float32 [14, 32768], P(None, ('lat', 'lon')), may hold values from 0.2 to 2
- sunlit: int32 [32768], P(('lat', 'lon')), may hold values from 0 to 1, as said below
- lw_table: bfloat16 [16, 3, 128, 128], P(None, None, 'lon'), may hold values from -0.3125 to 0.3125
- sw_table: bfloat16 [14, 3, 128, 128], P(None, None, 'lon'), may hold values from -0.3125 to 0.3125
Outputs:
- tendency: bfloat16 [65536, 128], P(('lat', 'lon'))
- gradient: bfloat16 [65536, 3, 128], P(('lat', 'lon'))
Inputs may be any that keep to these rules, and one draw needn't show every extreme that they name: In each device's block of 1024 radiation columns at most 640 are sunlit, and some device has exactly 640.
All inputs are finite; a program needn't handle non-finite values.
Results may differ from a plain program's by a relative error of at most 0.014.
Values may be sent and summed in bfloat16 or wider, within the bound.
A program may use at most 64 MiB of HBM per device.

v0:
```python
import functools

import jax
import jax.numpy as jnp
from jax import lax
from jax.experimental import pallas as pl
from jax.experimental.pallas import tpu as pltpu
from jax.sharding import PartitionSpec as P

BLOCK = 256


def lane_iota(rows, width):
    return lax.broadcasted_iota(jnp.int32, (rows, width), 1)


def row_iota(rows, width, start):
    return lax.broadcasted_iota(jnp.int32, (rows, width), 0) + start


def pick(hit):
    return jnp.where(hit, 1.0, 0.0).astype(jnp.bfloat16)


def blend(hit_first, hit_second, share):
    first = jnp.where(hit_first, share, 0.0)
    second = jnp.where(hit_second, 1.0 - share, 0.0)
    return (first + second).astype(jnp.bfloat16)


def dot(left, right):
    return lax.dot_general(left, right, (((1,), (0,)), ((), ())), preferred_element_type=jnp.float32)


def column_of(values):
    return jnp.transpose(jnp.broadcast_to(values, (8, values.shape[1])))[:, 0:1]


def radiate_kernel(
    lon_count,
    perm_ref,
    inc_ref,
    cot_ref,
    back_ref,
    back_w,
    lw_scale,
    sw_scale,
    sun_ref,
    lw_ref,
    sw_ref,
    coarse_ref,
    coarse_w,
    tend_done,
    grad_done,
    tend_in,
    grad_in,
    back,
    stacked,
    cot_out,
    cot_in,
    fields_out,
    fields_in,
    grad_out,
    tend_out,
    tabs,
    wide,
    flat,
    adj,
    heat,
    send_sem,
    recv_sem,
    tab_send,
    tab_recv,
):
    var_count, col_count, width = inc_ref.shape
    devices, segment = cot_out.shape[0], cot_out.shape[1]
    row_count = lw_scale.shape[1]
    lw_count = lw_ref.shape[0]
    band_count = lw_count + sw_ref.shape[0]
    per_block = BLOCK // segment
    blocks = col_count // BLOCK
    lat, lon = lax.axis_index("lat"), lax.axis_index("lon")
    me = lat * lon_count + lon
    parity = lax.rem(lon, 2)
    partner = lon + 1 - 2 * parity
    home = lax.div(me, per_block)

    def table_copy(source, slot, target, sem):
        return pltpu.make_async_remote_copy(
            src_ref=source,
            dst_ref=tabs.at[slot],
            send_sem=sem,
            recv_sem=tab_recv.at[slot],
            device_id=(lat, target),
            device_id_type=pl.DeviceIdType.MESH,
        )

    def copy(kind, source, landing, target, slot):
        return pltpu.make_async_remote_copy(
            src_ref=source,
            dst_ref=landing,
            send_sem=send_sem.at[kind, target],
            recv_sem=recv_sem.at[kind, slot],
            device_id=(lax.div(target, lon_count), lax.rem(target, lon_count)),
            device_id_type=pl.DeviceIdType.MESH,
        )

    def start_block(kind, source, landing, block):
        for k in range(per_block):
            target = block * per_block + k

            @pl.when(target != me)
            def _():
                copy(kind, source.at[target], landing.at[me], target, me).start()

    def wait_all(kind, landing):
        @pl.loop(1, devices)
        def _(k):
            source = lax.rem(me + k, devices)
            copy(kind, landing.at[source], landing.at[source], source, source).wait_recv()

    def wait_sent(kind, source):
        @pl.loop(1, devices)
        def _(k):
            target = lax.rem(me + k, devices)
            copy(kind, source.at[target], source.at[target], target, target).wait_send()

    def scale_of(rows):
        lit = sun_ref[:, rows].astype(jnp.float32)
        longwave, shortwave = jnp.transpose(lw_scale[:, rows]), jnp.transpose(sw_scale[:, rows] * lit)
        return [
            longwave[:, b : b + 1] if b < lw_count else shortwave[:, b - lw_count : b - lw_count + 1]
            for b in range(band_count)
        ]

    def turn(step):
        return lax.rem(step + home + 1, blocks)

    def split_rows(ref, block, values):
        for v in range(var_count):
            piece = values[:, v * width : (v + 1) * width]
            ref[pl.ds(block * per_block, per_block), v] = piece.reshape(per_block, segment, width)

    tabs[lon, pl.ds(0, lw_count)] = lw_ref[...]
    tabs[lon, pl.ds(lw_count, band_count - lw_count)] = sw_ref[...]
    stacked[:, pl.ds(0, width)] = cot_ref[...]
    for v in range(var_count):
        stacked[:, pl.ds((v + 1) * width, width)] = inc_ref[v]

    for j in range(1, lon_count // 2):
        target = lax.rem(lon + 2 * j, lon_count)
        table_copy(tabs.at[lon], lon, target, tab_send.at[0, target]).start()
    table_copy(tabs.at[lon], lon, partner, tab_send.at[0, partner]).start()

    @pl.loop(0, blocks)
    def _(step):
        block = turn(step)
        rows = pl.ds(pl.multiple_of(block * BLOCK, BLOCK), BLOCK)
        table = pick(column_of(perm_ref[:, rows]) == lane_iota(BLOCK, col_count))
        moved = dot(table, stacked[...]).astype(jnp.bfloat16)
        cot_out[pl.ds(block * per_block, per_block)] = moved[:, :width].reshape(per_block, segment, width)
        split_rows(fields_out, block, moved[:, width:])
        start_block(0, cot_out, cot_in, block)

    @pl.loop(0, blocks)
    def _(step):
        start_block(1, fields_out, fields_in, turn(step))

    cot_in[me] = cot_out[me]
    fields_in[me] = fields_out[me]
    for j in range(1, lon_count // 2):
        source = lax.rem(lon + 2 * j, lon_count)
        table_copy(tabs.at[source], source, source, tab_send.at[0, source]).wait_recv()
        table_copy(tabs.at[source], source, partner, tab_send.at[1, source]).start()
    wait_all(0, cot_in)
    for j in range(lon_count // 2):
        source = lax.rem(partner + 2 * j, lon_count)
        table_copy(tabs.at[source], source, source, tab_send.at[0, source]).wait_recv()
    depth = lw_ref.shape[2]
    for b in range(band_count):
        for v in range(var_count):
            part = tabs[:, b, v].reshape(lon_count * depth, width)
            wide[pl.ds(v * lon_count * depth, lon_count * depth), pl.ds(b * width, width)] = part

    @pl.loop(0, row_count // BLOCK)
    def _(step):
        start = pl.multiple_of(step * BLOCK, BLOCK)
        rows = pl.ds(start, BLOCK)
        spot = row_iota(BLOCK, col_count, start)
        table = blend(back_ref[0:1, :] == spot, back_ref[1:2, :] == spot, back_w[...])
        coarse = dot(table, cot_in[...].reshape(col_count, width))
        scale = scale_of(rows)
        lifted = jnp.concatenate([(scale[b] * coarse).astype(jnp.bfloat16) for b in range(band_count)], axis=1)
        out = lax.dot_general(lifted, wide[...], (((1,), (1,)), ((), ())), preferred_element_type=jnp.float32)
        adj[rows, :] = out.astype(jnp.bfloat16)

    @pl.loop(0, blocks)
    def _(step):
        block = turn(step)
        spot = row_iota(BLOCK, row_count, block * BLOCK)
        table = blend(coarse_ref[0:1, :] == spot, coarse_ref[1:2, :] == spot, coarse_w[...])
        split_rows(grad_out, block, dot(table, adj[...]).astype(jnp.bfloat16))
        start_block(2, grad_out, grad_in, block)

    grad_in[me] = grad_out[me]

    @pl.loop(0, blocks)
    def _(step):
        start = pl.multiple_of(step * BLOCK, BLOCK)
        back[pl.ds(start, BLOCK), :] = pick(perm_ref[...] == row_iota(BLOCK, col_count, start))

    wait_all(1, fields_in)
    for v in range(var_count):
        flat[:, pl.ds(v * width, width)] = fields_in[:, v].reshape(col_count, width)

    @pl.loop(0, row_count // BLOCK)
    def _(step):
        rows = pl.ds(pl.multiple_of(step * BLOCK, BLOCK), BLOCK)
        spot = lane_iota(BLOCK, col_count)
        first, second = column_of(coarse_ref[0:1, rows]), column_of(coarse_ref[1:2, rows])
        table = blend(first == spot, second == spot, column_of(coarse_w[:, rows]))
        coarse = dot(table, flat[...]).astype(jnp.bfloat16)
        scale = scale_of(rows)
        total = jnp.zeros((BLOCK, width), jnp.float32)
        for b in range(0, band_count, 2):
            pair = dot(coarse, wide[:, b * width : (b + 2) * width])
            total = total + scale[b] * pair[:, :width] + scale[b + 1] * pair[:, width:]
        heat[rows, :] = total.astype(jnp.bfloat16)

    @pl.loop(0, blocks)
    def _(step):
        block = turn(step)
        rows = pl.ds(pl.multiple_of(block * BLOCK, BLOCK), BLOCK)
        spot = lane_iota(BLOCK, row_count)
        first, second = column_of(back_ref[0:1, rows]), column_of(back_ref[1:2, rows])
        table = blend(first == spot, second == spot, column_of(back_w[:, rows]))
        moved = dot(table, heat[...]).astype(jnp.bfloat16)
        tend_out[pl.ds(block * per_block, per_block)] = moved.reshape(per_block, segment, width)
        start_block(3, tend_out, tend_in, block)

    tend_in[me] = tend_out[me]
    for j in range(1, lon_count // 2):
        other = lax.rem(lon + 2 * j, lon_count)
        table_copy(tabs.at[lon], other, other, tab_send.at[0, other]).wait_send()
        table_copy(tabs.at[lon], other, other, tab_send.at[1, other]).wait_send()
    table_copy(tabs.at[lon], partner, partner, tab_send.at[0, partner]).wait_send()
    wait_all(2, grad_in)
    for v in range(var_count):
        flat[:, pl.ds(v * width, width)] = grad_in[:, v].reshape(col_count, width)

    @pl.loop(0, blocks)
    def _(step):
        rows = pl.ds(pl.multiple_of(step * BLOCK, BLOCK), BLOCK)
        moved = dot(back[rows, :], flat[...]).astype(jnp.bfloat16)
        for v in range(var_count):
            grad_done[v, rows, :] = moved[:, v * width : (v + 1) * width]

    wait_all(3, tend_in)

    @pl.loop(0, blocks)
    def _(step):
        rows = pl.ds(pl.multiple_of(step * BLOCK, BLOCK), BLOCK)
        tend_done[rows, :] = dot(back[rows, :], tend_in[...].reshape(col_count, width)).astype(jnp.bfloat16)

    wait_sent(0, cot_out)
    wait_sent(1, fields_out)
    wait_sent(2, grad_out)
    wait_sent(3, tend_out)


def run(kernel, outs, scratch, flops, args, sems=(), talks=False):
    shapes = [jax.ShapeDtypeStruct(shape, jnp.bfloat16) for shape in outs]
    vmem = pl.BlockSpec(memory_space=pltpu.VMEM)
    return pl.pallas_call(
        kernel,
        out_shape=shapes,
        in_specs=[vmem] * len(args),
        out_specs=[vmem] * len(outs),
        scratch_shapes=[pltpu.VMEM(shape, jnp.bfloat16) for shape in scratch] + [pltpu.SemaphoreType.DMA(shape) for shape in sems],
        compiler_params=pltpu.CompilerParams(vmem_limit_bytes=56 * 1024 * 1024, has_side_effects=talks),
        cost_estimate=pl.CostEstimate(flops=flops, bytes_accessed=4 << 20, transcendentals=0),
    )(*args)


def local(
    increments,
    cotangent,
    owner_perm,
    coarse_index,
    coarse_weight,
    back_index,
    back_weight,
    lw_scale,
    sw_scale,
    sunlit,
    lw_table,
    sw_table,
    *,
    devices,
    lon_count,
):
    col_count, var_count, width = increments.shape
    row_count = coarse_weight.shape[0]
    segment = col_count // devices
    thin, split = (devices, segment, width), (devices, var_count, segment, width)
    flat_width = var_count * width
    bands = lw_table.shape[0] + sw_table.shape[0]
    planes = jnp.transpose(increments, (1, 0, 2))
    stack = (col_count, (var_count + 1) * width)
    back_w, coarse_w = back_weight[None, :], coarse_weight[None, :]
    tendency, gradient = run(
        functools.partial(radiate_kernel, lon_count),
        [(col_count, width), (var_count, col_count, width)],
        [
            thin,
            split,
            (col_count, col_count),
            stack,
            thin,
            thin,
            split,
            split,
            split,
            thin,
            (lon_count, bands) + lw_table.shape[1:],
            (flat_width, bands * width),
            (col_count, flat_width),
            (row_count, flat_width),
            (row_count, width),
        ],
        6 * row_count * bands * flat_width * width,
        (
            owner_perm,
            planes,
            cotangent,
            back_index,
            back_w,
            lw_scale,
            sw_scale,
            sunlit[None, :],
            lw_table,
            sw_table,
            coarse_index,
            coarse_w,
        ),
        sems=((4, devices), (4, devices), (2, lon_count), (lon_count,)),
        talks=True,
    )
    return (tendency, jnp.transpose(gradient, (1, 0, 2)))


def solution(mesh):
    in_specs = (
        P(("lat", "lon"), None, None),
        P(("lat", "lon"), None),
        P(("lat", "lon"), None),
        P(None, ("lat", "lon")),
        P(("lat", "lon")),
        P(None, ("lat", "lon")),
        P(("lat", "lon")),
        P(None, ("lat", "lon")),
        P(None, ("lat", "lon")),
        P(("lat", "lon")),
        P(None, None, "lon", None),
        P(None, None, "lon", None),
    )
    out_specs = (P(("lat", "lon"), None), P(("lat", "lon"), None, None))
    devices = mesh.shape["lat"] * mesh.shape["lon"]

    def body(*args):
        return local(*args, devices=devices, lon_count=mesh.shape["lon"])

    return jax.shard_map(body, mesh=mesh, in_specs=in_specs, out_specs=out_specs, check_vma=False)
```

profile of v0, /device:TPU:15, one launch (start us, length us, event | category | flops | bytes accessed | tf_op | source)
XLA Modules:
  0.0 121.0 jit_solution(16821641136035746337)
XLA Ops:
  0.6 115.8 %shard_map.131 = (bf16[2048,128]{1,0:T(8,128)(2,1)}, bf16[3,2048,128]{2,1,0:T(8,128)(2,1)}) custom-call(s32[1,2048]{1,0:T(1,128)} %perm_ref.1, bf16[3,2048,128]{2,1,0:T(8,128)(2,1)} %bitcast.6, bf16[2048,128]{1,0:T(8,128)(2,1)} %cot_ref.1, s32[2,2048]{1,0:T(2,128)} %back_ref.1, f32[1,2048]{1,0:T(1,128)} %bitcast.7, f32[16,1024]{1,0:T(8,128)} %lw_scale.1, ...), custom_call_target="tpu_custom_call" | custom-call | flops 9059696640 | bytes 4194304 | tf_op jit(solution)/shard_map/pallas_call | solution.py:274
  116.5 1.9 %copy.16 = bf16[2048,128]{1,0:T(8,128)(2,1)} copy(bf16[2048,128]{1,0:T(8,128)(2,1)} %get-tuple-element.8) | data formatting | bytes 1048576
  118.4 2.7 %copy.17 = bf16[2048,3,128]{2,0,1:T(8,128)(2,1)} copy(bf16[2048,3,128]{2,0,1:T(8,128)(2,1)} %bitcast.5) | data formatting | bytes 3145728
where the time goes:
time: 121 us
  Pallas kernels  116 us (96%)
  local copies, waits for them, and re-layouts  4.52 us (4%)
    pallas_call x1, Pallas kernels, run(): pl.pallas_call(kernel, out_shape=shapes, in_specs=[vmem] * len(args), out...  116 us
    unnamed x2, local copies, waits for them, and re-layouts  4.52 us

commit v1 on v0

v1 whole, which is shorter than its diff:
```python
import jax
import jax.numpy as jnp
from jax import lax
from jax.experimental import pallas as pl
from jax.experimental.pallas import tpu as pltpu
from jax.sharding import PartitionSpec as P

BLOCK = 256


def lane_iota(rows, width):
    return lax.broadcasted_iota(jnp.int32, (rows, width), 1)


def row_iota(rows, width, start):
    return lax.broadcasted_iota(jnp.int32, (rows, width), 0) + start


def pick(hit):
    return jnp.where(hit, 1.0, 0.0).astype(jnp.bfloat16)


def blend(hit_first, hit_second, share):
    first = jnp.where(hit_first, share, 0.0)
    second = jnp.where(hit_second, 1.0 - share, 0.0)
    return (first + second).astype(jnp.bfloat16)


def dot(left, right):
    return lax.dot_general(left, right, (((1,), (0,)), ((), ())), preferred_element_type=jnp.float32)


def column_of(values):
    return jnp.transpose(jnp.broadcast_to(values, (8, values.shape[1])))[:, 0:1]


def radiate_kernel(
    perm_ref,
    inc_ref,
    cot_ref,
    back_ref,
    back_w,
    lw_scale,
    sw_scale,
    sun_ref,
    lw_ref,
    sw_ref,
    coarse_ref,
    coarse_w,
    tend_done,
    grad_done,
    back,
    stacked,
    cot_out,
    cot_in,
    fields_out,
    fields_in,
    grad_out,
    grad_in,
    tend_out,
    tend_in,
    tabs,
    wide,
    adj,
    heat,
    up_out,
    up_in,
    down_out,
    down_in,
    own,
    scale_in,
    coarse_in,
    share_in,
    back_in,
    back_share,
    send_sem,
    recv_sem,
    chain_send,
    chain_recv,
    meta_send,
    meta_recv,
    tab_send,
    tab_recv,
):
    var_count, col_count, width = inc_ref.shape
    planes, lon_count, segment = cot_out.shape[0], cot_out.shape[1], cot_out.shape[2]
    part = lon_count * segment
    row_count = lw_scale.shape[1]
    lw_count = lw_ref.shape[0]
    band_count = lw_count + sw_ref.shape[0]
    flat_width = var_count * width
    per_block = BLOCK // segment
    part_blocks = part // BLOCK
    row_blocks = row_count // BLOCK
    lat, lon = lax.axis_index("lat"), lax.axis_index("lon")
    parity = lax.rem(lon, 2)
    partner = lon + 1 - 2 * parity
    home = lax.div(lon, per_block)
    groups = (pl.ds(0, lw_count), pl.ds(lw_count, band_count - lw_count))

    def remote(source, landing, send, recv, target_lat, target_lon):
        return pltpu.make_async_remote_copy(
            src_ref=source,
            dst_ref=landing,
            send_sem=send,
            recv_sem=recv,
            device_id=(target_lat, target_lon),
            device_id_type=pl.DeviceIdType.MESH,
        )

    def table_copy(group, slot, target, hop):
        piece = tabs.at[slot, groups[group]]
        return remote(piece, piece, tab_send.at[group, hop, target], tab_recv.at[group, slot], lat, target)

    def copy(kind, source, landing, block, target, slot):
        return remote(source, landing, send_sem.at[kind, block, target], recv_sem.at[kind, block, slot], lat, target)

    def start_block(kind, source, landing, block, step):
        for k in range(per_block):
            target = step * per_block + k

            @pl.when(target != lon)
            def _():
                copy(kind, source.at[block, target], landing.at[block, lon], block, target, lon).start()

            @pl.when(target == lon)
            def _():
                landing[block, lon] = source[block, lon]

    def wait_block(kind, landing, block):
        @pl.loop(1, lon_count)
        def _(k):
            source = lax.rem(lon + k, lon_count)
            piece = landing.at[block, source]
            copy(kind, piece, piece, block, source, source).wait_recv()

    def wait_sent(kind, source):
        @pl.loop(0, planes)
        def _(block):
            @pl.loop(1, lon_count)
            def _(k):
                target = lax.rem(lon + k, lon_count)
                piece = source.at[block, target]
                copy(kind, piece, piece, block, target, target).wait_send()

    def meta_copy(kind, target, slot):
        span = pl.ds(pl.multiple_of(target * part, part), part)
        source, landing = (
            (back_ref.at[:, span], back_in.at[slot]),
            (back_w.at[:, span], back_share.at[slot]),
            (coarse_ref, coarse_in.at[slot]),
            (coarse_w, share_in.at[slot]),
            (scale_in.at[slot], scale_in.at[slot]),
        )[kind]
        return remote(source, landing, meta_send.at[kind, target], meta_recv.at[kind, slot], target, lon)

    def wait_meta(kinds):
        @pl.loop(1, planes)
        def _(k):
            source = lax.rem(lat + k, planes)
            for kind in kinds:
                meta_copy(kind, source, source).wait_recv()

    def chain_copy(kind, upward, block):
        out, landing, way = (up_out, up_in, 0) if upward else (down_out, down_in, 1)
        target = lat + 1 if upward else lat - 1
        piece, spot = out.at[kind, block], landing.at[kind, block]
        return remote(piece, spot, chain_send.at[kind, way, block], chain_recv.at[kind, way, block], target, lon)

    def chain_begin(kind, block):
        if planes == 1:
            return

        @pl.when(lat == 0)
        def _():
            up_out[kind, block] = own[kind, block].astype(jnp.bfloat16)
            chain_copy(kind, True, block).start()

        @pl.when(lat == planes - 1)
        def _():
            down_out[kind, block] = own[kind, block].astype(jnp.bfloat16)
            chain_copy(kind, False, block).start()

    def chain_hop(kind, hop, block):
        @pl.when(lat == hop)
        def _():
            chain_copy(kind, True, block).wait_recv()
            up_out[kind, block] = (own[kind, block] + up_in[kind, block].astype(jnp.float32)).astype(jnp.bfloat16)
            chain_copy(kind, True, block).start()

        @pl.when(lat == planes - 1 - hop)
        def _():
            chain_copy(kind, False, block).wait_recv()
            down_out[kind, block] = (own[kind, block] + down_in[kind, block].astype(jnp.float32)).astype(jnp.bfloat16)
            chain_copy(kind, False, block).start()

    def chain_after(kind, block):
        for hop in range(1, planes - 1):

            @pl.when(block >= hop - 1)
            def _():
                chain_hop(kind, hop, block - hop + 1)

    def chain_rest(kind):
        for late in range(planes, 2 * planes - 2):
            for hop in range(1, planes - 1):
                if 0 <= late - hop + 1 < planes:
                    chain_hop(kind, hop, late - hop + 1)

    def chain_ready(kind, block):
        if planes == 1:
            return

        @pl.when(lat == 0)
        def _():
            chain_copy(kind, False, block).wait_recv()

        @pl.when(lat == planes - 1)
        def _():
            chain_copy(kind, True, block).wait_recv()

    def chain_total(kind, block, rows):
        ends = up_in[kind, block, rows, :].astype(jnp.float32) + down_in[kind, block, rows, :].astype(jnp.float32)
        return own[kind, block, rows, :] + ends

    def chain_sent(kind):
        @pl.loop(0, planes)
        def _(block):
            @pl.when(lat < planes - 1)
            def _():
                chain_copy(kind, True, block).wait_send()

            @pl.when(lat > 0)
            def _():
                chain_copy(kind, False, block).wait_send()

    def scale_of(block, rows):
        turned = jnp.transpose(scale_in[block, :, rows])
        return [turned[:, b : b + 1] for b in range(band_count)]

    def sub_rows(step):
        return pl.ds(pl.multiple_of(step * BLOCK, BLOCK), BLOCK)

    tabs[lon, groups[0]] = lw_ref[...]
    tabs[lon, groups[1]] = sw_ref[...]
    for j in range(1, lon_count // 2):
        target = lax.rem(lon + 2 * j, lon_count)
        table_copy(0, lon, target, 0).start()
    table_copy(0, lon, partner, 0).start()

    scale_in[lat, pl.ds(0, lw_count)] = lw_scale[...]
    scale_in[lat, pl.ds(lw_count, band_count - lw_count)] = sw_scale[...] * sun_ref[...].astype(jnp.float32)
    scale_in[lat, pl.ds(band_count, scale_in.shape[1] - band_count)] = jnp.zeros(
        (scale_in.shape[1] - band_count, row_count), jnp.float32
    )
    span = pl.ds(pl.multiple_of(lat * part, part), part)
    back_in[lat] = back_ref[:, span]
    back_share[lat] = back_w[:, span]
    coarse_in[lat] = coarse_ref[...]
    share_in[lat] = coarse_w[...]

    @pl.loop(1, planes)
    def _(k):
        for kind in range(5):
            meta_copy(kind, lax.rem(lat + k, planes), lat).start()

    @pl.when(lat == 0)
    def _():
        up_in[...] = jnp.zeros_like(up_in)

    @pl.when(lat == planes - 1)
    def _():
        down_in[...] = jnp.zeros_like(down_in)

    stacked[:, pl.ds(0, width)] = cot_ref[...]
    for v in range(var_count):
        stacked[:, pl.ds((v + 1) * width, width)] = inc_ref[v]

    @pl.loop(0, planes)
    def _(block):
        @pl.loop(0, part_blocks)
        def _(turn):
            step = lax.rem(turn + home + 1, part_blocks)
            rows = sub_rows(block * part_blocks + step)
            table = pick(column_of(perm_ref[:, rows]) == lane_iota(BLOCK, col_count))
            moved = dot(table, stacked[...]).astype(jnp.bfloat16)
            spot = pl.ds(step * per_block, per_block)
            cot_out[block, spot] = moved[:, :width].reshape(per_block, segment, width)
            fields_out[block, spot] = moved[:, width:].reshape(per_block, segment, flat_width)
            start_block(0, cot_out, cot_in, block, step)

    for j in range(1, lon_count // 2):
        target = lax.rem(lon + 2 * j, lon_count)
        table_copy(1, lon, target, 0).start()
    table_copy(1, lon, partner, 0).start()

    @pl.loop(0, planes)
    def _(block):
        @pl.loop(0, part_blocks)
        def _(turn):
            start_block(1, fields_out, fields_in, block, lax.rem(turn + home + 1, part_blocks))

    wait_meta((0, 1))

    @pl.loop(0, planes)
    def _(block):
        wait_block(0, cot_in, block)

        @pl.loop(0, row_blocks)
        def _(step):
            rows = sub_rows(step)
            spot = row_iota(BLOCK, part, step * BLOCK)
            index = back_in[block]
            table = blend(index[0:1, :] == spot, index[1:2, :] == spot, back_share[block])
            own[0, block, rows, :] = dot(table, cot_in[block].reshape(part, width))

        chain_begin(0, block)

    for group in range(2):
        for j in range(1, lon_count // 2):
            source = lax.rem(lon + 2 * j, lon_count)
            table_copy(group, source, source, 0).wait_recv()
            table_copy(group, source, partner, 1 + j).start()

    @pl.loop(0, col_count // BLOCK)
    def _(step):
        back[sub_rows(step), :] = pick(perm_ref[...] == row_iota(BLOCK, col_count, step * BLOCK))

    for group in range(2):
        for j in range(lon_count // 2):
            source = lax.rem(partner + 2 * j, lon_count)
            table_copy(group, source, source, 0).wait_recv()
    depth = lw_ref.shape[2]
    for b in range(band_count):
        for v in range(var_count):
            piece = tabs[:, b, v].reshape(lon_count * depth, width)
            wide[pl.ds(v * lon_count * depth, lon_count * depth), pl.ds(b * width, width)] = piece
    wait_meta((2, 3, 4))

    @pl.loop(0, planes)
    def _(block):
        wait_block(1, fields_in, block)

        @pl.loop(0, row_blocks)
        def _(step):
            rows = sub_rows(step)
            spot = lane_iota(BLOCK, part) + lat * part
            first, second = column_of(coarse_in[block, 0:1, rows]), column_of(coarse_in[block, 1:2, rows])
            table = blend(first == spot, second == spot, column_of(share_in[block, :, rows]))
            coarse = dot(table, fields_in[block].reshape(part, flat_width)).astype(jnp.bfloat16)
            scale = scale_of(block, rows)
            total = jnp.zeros((BLOCK, width), jnp.float32)
            for b in range(0, band_count, 2):
                pair = dot(coarse, wide[:, b * width : (b + 2) * width])
                total = total + scale[b] * pair[:, :width] + scale[b + 1] * pair[:, width:]
            own[1, block, rows, :] = total

        chain_begin(1, block)
        chain_after(0, block)

    chain_rest(0)

    @pl.loop(0, planes)
    def _(block):
        chain_ready(0, block)

        @pl.loop(0, row_blocks)
        def _(step):
            rows = sub_rows(step)
            coarse = chain_total(0, block, rows)
            scale = scale_of(block, rows)
            lifted = jnp.concatenate([(scale[b] * coarse).astype(jnp.bfloat16) for b in range(band_count)], axis=1)
            out = lax.dot_general(lifted, wide[...], (((1,), (1,)), ((), ())), preferred_element_type=jnp.float32)
            adj[rows, :] = out.astype(jnp.bfloat16)

        @pl.loop(0, part_blocks)
        def _(turn):
            step = lax.rem(turn + home + 1, part_blocks)
            spot = row_iota(BLOCK, row_count, lat * part + step * BLOCK)
            index = coarse_in[block]
            table = blend(index[0:1, :] == spot, index[1:2, :] == spot, share_in[block])
            moved = dot(table, adj[...]).astype(jnp.bfloat16)
            grad_out[block, pl.ds(step * per_block, per_block)] = moved.reshape(per_block, segment, flat_width)
            start_block(2, grad_out, grad_in, block, step)

        chain_after(1, block)

    chain_rest(1)

    @pl.loop(0, planes)
    def _(block):
        chain_ready(1, block)
        heat[...] = chain_total(1, block, pl.ds(0, row_count)).astype(jnp.bfloat16)

        @pl.loop(0, part_blocks)
        def _(turn):
            step = lax.rem(turn + home + 1, part_blocks)
            rows = sub_rows(step)
            spot = lane_iota(BLOCK, row_count)
            first, second = column_of(back_in[block, 0:1, rows]), column_of(back_in[block, 1:2, rows])
            table = blend(first == spot, second == spot, column_of(back_share[block, :, rows]))
            moved = dot(table, heat[...]).astype(jnp.bfloat16)
            tend_out[block, pl.ds(step * per_block, per_block)] = moved.reshape(per_block, segment, width)
            start_block(3, tend_out, tend_in, block, step)

    @pl.loop(0, planes)
    def _(block):
        wait_block(2, grad_in, block)

    @pl.loop(0, col_count // BLOCK)
    def _(step):
        rows = sub_rows(step)
        moved = dot(back[rows, :], grad_in[...].reshape(col_count, flat_width)).astype(jnp.bfloat16)
        for v in range(var_count):
            grad_done[v, rows, :] = moved[:, v * width : (v + 1) * width]

    @pl.loop(0, planes)
    def _(block):
        wait_block(3, tend_in, block)

    @pl.loop(0, col_count // BLOCK)
    def _(step):
        rows = sub_rows(step)
        tend_done[rows, :] = dot(back[rows, :], tend_in[...].reshape(col_count, width)).astype(jnp.bfloat16)

    for group in range(2):
        for j in range(1, lon_count // 2):
            other = lax.rem(lon + 2 * j, lon_count)
            table_copy(group, lon, other, 0).wait_send()
            table_copy(group, other, partner, 1 + j).wait_send()
        table_copy(group, lon, partner, 0).wait_send()

    @pl.loop(1, planes)
    def _(k):
        for kind in range(5):
            meta_copy(kind, lax.rem(lat + k, planes), lat).wait_send()

    chain_sent(0)
    chain_sent(1)
    wait_sent(0, cot_out)
    wait_sent(1, fields_out)
    wait_sent(2, grad_out)
    wait_sent(3, tend_out)


def run(kernel, outs, scratch, flops, args, sems):
    shapes = [jax.ShapeDtypeStruct(shape, jnp.bfloat16) for shape in outs]
    vmem = pl.BlockSpec(memory_space=pltpu.VMEM)
    return pl.pallas_call(
        kernel,
        out_shape=shapes,
        in_specs=[vmem] * len(args),
        out_specs=[vmem] * len(outs),
        scratch_shapes=[pltpu.VMEM(shape, kind) for shape, kind in scratch] + [pltpu.SemaphoreType.DMA(shape) for shape in sems],
        compiler_params=pltpu.CompilerParams(vmem_limit_bytes=56 * 1024 * 1024, has_side_effects=True),
        cost_estimate=pl.CostEstimate(flops=flops, bytes_accessed=4 << 20, transcendentals=0),
    )(*args)


def local(
    increments,
    cotangent,
    owner_perm,
    coarse_index,
    coarse_weight,
    back_index,
    back_weight,
    lw_scale,
    sw_scale,
    sunlit,
    lw_table,
    sw_table,
    *,
    planes,
    lon_count,
):
    col_count, var_count, width = increments.shape
    row_count = coarse_weight.shape[0]
    segment = col_count // (planes * lon_count)
    part = lon_count * segment
    flat_width = var_count * width
    thin, thick = (planes, lon_count, segment, width), (planes, lon_count, segment, flat_width)
    bands = lw_table.shape[0] + sw_table.shape[0]
    scale_rows = -(-(bands + 1) // 8) * 8
    wire = (2, planes, row_count, width)
    half, full, whole = jnp.bfloat16, jnp.float32, jnp.int32
    tendency, gradient = run(
        radiate_kernel,
        [(col_count, width), (var_count, col_count, width)],
        [
            ((col_count, col_count), half),
            ((col_count, (var_count + 1) * width), half),
            (thin, half),
            (thin, half),
            (thick, half),
            (thick, half),
            (thick, half),
            (thick, half),
            (thin, half),
            (thin, half),
            ((lon_count, bands) + lw_table.shape[1:], half),
            ((flat_width, bands * width), half),
            ((row_count, flat_width), half),
            ((row_count, width), half),
            (wire, half),
            (wire, half),
            (wire, half),
            (wire, half),
            (wire, full),
            ((planes, scale_rows, row_count), full),
            ((planes, 2, row_count), whole),
            ((planes, 1, row_count), full),
            ((planes, 2, part), whole),
            ((planes, 1, part), full),
        ],
        6 * planes * row_count * bands * flat_width * width,
        (
            owner_perm,
            jnp.transpose(increments, (1, 0, 2)),
            cotangent,
            back_index,
            back_weight[None, :],
            lw_scale,
            sw_scale,
            sunlit[None, :],
            lw_table,
            sw_table,
            coarse_index,
            coarse_weight[None, :],
        ),
        (
            (4, planes, lon_count),
            (4, planes, lon_count),
            (2, 2, planes),
            (2, 2, planes),
            (5, planes),
            (5, planes),
            (2, lon_count // 2 + 1, lon_count),
            (2, lon_count),
        ),
    )
    return (tendency, jnp.transpose(gradient, (1, 0, 2)))


def solution(mesh):
    in_specs = (
        P(("lat", "lon"), None, None),
        P(("lat", "lon"), None),
        P(("lat", "lon"), None),
        P(None, ("lat", "lon")),
        P(("lat", "lon")),
        P(None, ("lat", "lon")),
        P(("lat", "lon")),
        P(None, ("lat", "lon")),
        P(None, ("lat", "lon")),
        P(("lat", "lon")),
        P(None, None, "lon", None),
        P(None, None, "lon", None),
    )
    out_specs = (P(("lat", "lon"), None), P(("lat", "lon"), None, None))

    def body(*args):
        return local(*args, planes=mesh.shape["lat"], lon_count=mesh.shape["lon"])

    return jax.shard_map(body, mesh=mesh, in_specs=in_specs, out_specs=out_specs, check_vma=False)
```

time: 121 us -> 140 us (1.16)
  the two profiles are of different devices: /device:TPU:15 before, /device:TPU:0 now
where the time goes in v1:
time: 140 us
  Pallas kernels  135 us (96%)
  local copies, waits for them, and re-layouts  4.52 us (3%)
    pallas_call x1, Pallas kernels, run(): pl.pallas_call(kernel, out_shape=shapes, in_specs=[vmem] * len(args), out...  135 us
    unnamed x2, local copies, waits for them, and re-layouts  4.52 us

profile of v1, /device:TPU:0, one launch (start us, length us, event | category | flops | bytes accessed | tf_op | source)
XLA Modules:
  0.0 140.0 jit_solution(12236062338417640557)
XLA Ops:
  0.6 134.9 %shard_map.131 = (bf16[2048,128]{1,0:T(8,128)(2,1)}, bf16[3,2048,128]{2,1,0:T(8,128)(2,1)}) custom-call(s32[1,2048]{1,0:T(1,128)} %perm_ref.1, bf16[3,2048,128]{2,1,0:T(8,128)(2,1)} %bitcast.6, bf16[2048,128]{1,0:T(8,128)(2,1)} %cot_ref.1, s32[2,2048]{1,0:T(2,128)} %back_ref.1, f32[1,2048]{1,0:T(1,128)} %bitcast.7, f32[16,1024]{1,0:T(8,128)} %lw_scale.1, ...), custom_call_target="tpu_custom_call" | custom-call | flops 36238786560 | bytes 4194304 | tf_op jit(solution)/shard_map/pallas_call | solution.py:449
  135.5 1.9 %copy.16 = bf16[2048,128]{1,0:T(8,128)(2,1)} copy(bf16[2048,128]{1,0:T(8,128)(2,1)} %get-tuple-element.8) | data formatting | bytes 1048576
  137.4 2.7 %copy.17 = bf16[2048,3,128]{2,0,1:T(8,128)(2,1)} copy(bf16[2048,3,128]{2,0,1:T(8,128)(2,1)} %bitcast.5) | data formatting | bytes 3145728

commit v2 on v1

v2 whole, which is shorter than its diff:
```python
import jax
import jax.numpy as jnp
from jax import lax
from jax.experimental import pallas as pl
from jax.experimental.pallas import tpu as pltpu
from jax.sharding import PartitionSpec as P

BLOCK = 256
FINAL = 512
BUNCH = 3
WIDE_SUMS = 4096


def lane_iota(rows, width):
    return lax.broadcasted_iota(jnp.int32, (rows, width), 1)


def row_iota(rows, width, start):
    return lax.broadcasted_iota(jnp.int32, (rows, width), 0) + start


def pick(hit):
    return jnp.where(hit, 1.0, 0.0).astype(jnp.bfloat16)


def blend(hit_first, hit_second, share):
    first = jnp.where(hit_first, share, 0.0)
    second = jnp.where(hit_second, 1.0 - share, 0.0)
    return (first + second).astype(jnp.bfloat16)


def dot(left, right):
    return lax.dot_general(left, right, (((1,), (0,)), ((), ())), preferred_element_type=jnp.float32)


def column_of(values):
    return jnp.transpose(jnp.broadcast_to(values, (8, values.shape[1])))[:, 0:1]


def radiate_kernel(
    perm_ref,
    inc_ref,
    cot_ref,
    back_ref,
    back_w,
    lw_scale,
    sw_scale,
    sun_ref,
    lw_ref,
    sw_ref,
    coarse_ref,
    coarse_w,
    result_in,
    stacked,
    cot_out,
    cot_in,
    fields_out,
    fields_in,
    grad_out,
    tend_out,
    tabs,
    wide,
    turned,
    ctab,
    btab,
    fields_t,
    adj,
    heat,
    up_out,
    up_in,
    down_out,
    down_in,
    own,
    scale_in,
    coarse_in,
    share_in,
    back_in,
    back_share,
    send_sem,
    recv_sem,
    chain_send,
    chain_recv,
    meta_send,
    meta_recv,
    tab_send,
    tab_recv,
):
    var_count, col_count, width = inc_ref.shape
    planes, lon_count, segment = cot_out.shape[0], cot_out.shape[1], cot_out.shape[2]
    part = lon_count * segment
    row_count = lw_scale.shape[1]
    lw_count = lw_ref.shape[0]
    band_count = lw_count + sw_ref.shape[0]
    flat_width = var_count * width
    row_blocks = row_count // BLOCK
    units = planes * row_blocks
    lat, lon = lax.axis_index("lat"), lax.axis_index("lon")
    parity = lax.rem(lon, 2)
    partner = lon + 1 - 2 * parity
    groups = (pl.ds(0, lw_count), pl.ds(lw_count, band_count - lw_count))

    def remote(source, landing, send, recv, target_lat, target_lon):
        return pltpu.make_async_remote_copy(
            src_ref=source,
            dst_ref=landing,
            send_sem=send,
            recv_sem=recv,
            device_id=(target_lat, target_lon),
            device_id_type=pl.DeviceIdType.MESH,
        )

    def table_copy(group, slot, target, hop):
        piece = tabs.at[slot, groups[group]]
        return remote(piece, piece, tab_send.at[group, hop, target], tab_recv.at[group, slot], lat, target)

    quad = lon_count == 8
    if quad:
        across = lon + 2 - 4 * lax.rem(lax.div(lon, 2), 2)
        along = lon + 4 - 8 * lax.div(lon, 4)
        near, far = (across, along), across + along - lon
    else:
        near, far = tuple(lax.rem(lon + 2 * j, lon_count) for j in range(1, lon_count // 2)), None

    def relay(group, done):
        @pl.when(parity == 0)
        def _():
            piece = table_copy(group, near[0], near[1], 1)
            piece.wait_send() if done else piece.start()

        @pl.when(parity == 1)
        def _():
            piece = table_copy(group, near[1], near[0], 1)
            piece.wait_send() if done else piece.start()

    def table_start(group):
        for target in near + (partner,):
            table_copy(group, lon, target, 0).start()

    def table_relay(group):
        for source in near:
            table_copy(group, source, source, 0).wait_recv()
        if quad:
            relay(group, False)
        for j, source in enumerate(near):
            table_copy(group, source, partner, 2 + j).start()

    def table_finish(group):
        if quad:
            table_copy(group, far, far, 0).wait_recv()
            table_copy(group, far, partner, 2 + len(near)).start()

    def table_wait(group):
        for j in range(lon_count // 2):
            source = lax.rem(partner + 2 * j, lon_count)
            table_copy(group, source, source, 0).wait_recv()

    def table_sent(group):
        for target in near + (partner,):
            table_copy(group, lon, target, 0).wait_send()
        if quad:
            relay(group, True)
        for j, source in enumerate(near + ((far,) if quad else ())):
            table_copy(group, source, partner, 2 + j).wait_send()

    def copy(kind, source, landing, block, target, slot):
        return remote(source, landing, send_sem.at[kind, block, target], recv_sem.at[kind, block, slot], lat, target)

    def start_block(kind, source, landing, block):
        landing.at[block, lon][...] = source[block, lon]

        @pl.loop(1, lon_count)
        def _(k):
            target = lax.rem(lon + k, lon_count)
            copy(kind, source.at[block, target], landing.at[block, lon], block, target, lon).start()

    def wait_block(kind, landing, block):
        @pl.loop(1, lon_count)
        def _(k):
            source = lax.rem(lon + k, lon_count)
            piece = landing.at[block, source]
            copy(kind, piece, piece, block, source, source).wait_recv()

    def wait_sent(kind, source):
        @pl.loop(0, planes)
        def _(block):
            @pl.loop(1, lon_count)
            def _(k):
                target = lax.rem(lon + k, lon_count)
                piece = source.at[block, target]
                copy(kind, piece, piece, block, target, target).wait_send()

    def meta_copy(kind, target, slot):
        span = pl.ds(pl.multiple_of(target * part, part), part)
        source, landing = (
            (back_ref.at[:, span], back_in.at[slot]),
            (back_w.at[:, span], back_share.at[slot]),
            (coarse_ref, coarse_in.at[slot]),
            (coarse_w, share_in.at[slot]),
            (scale_in.at[slot], scale_in.at[slot]),
        )[kind]
        return remote(source, landing, meta_send.at[kind, target], meta_recv.at[kind, slot], target, lon)

    def wait_meta(kinds):
        @pl.loop(1, planes)
        def _(k):
            source = lax.rem(lat + k, planes)
            for kind in kinds:
                meta_copy(kind, source, source).wait_recv()

    def chain_copy(kind, upward, unit):
        out, landing, way = (up_out, up_in, 0) if upward else (down_out, down_in, 1)
        target = lat + 1 if upward else lat - 1
        piece, spot = out.at[kind, unit], landing.at[kind, unit]
        return remote(piece, spot, chain_send.at[kind, way, unit], chain_recv.at[kind, way, unit], target, lon)

    def chain_begin(kind, unit):
        if planes == 1:
            return

        @pl.when(lat == 0)
        def _():
            up_out[kind, unit] = own[kind, unit].astype(jnp.bfloat16)
            chain_copy(kind, True, unit).start()

        @pl.when(lat == planes - 1)
        def _():
            down_out[kind, unit] = own[kind, unit].astype(jnp.bfloat16)
            chain_copy(kind, False, unit).start()

    def chain_hop(kind, hop, unit):
        @pl.when((lat == hop) & (unit >= 0) & (unit < units))
        def _():
            chain_copy(kind, True, unit).wait_recv()
            up_out[kind, unit] = (own[kind, unit].astype(jnp.float32) + up_in[kind, unit].astype(jnp.float32)).astype(jnp.bfloat16)
            chain_copy(kind, True, unit).start()

        @pl.when((lat == planes - 1 - hop) & (unit >= 0) & (unit < units))
        def _():
            chain_copy(kind, False, unit).wait_recv()
            down_out[kind, unit] = (own[kind, unit].astype(jnp.float32) + down_in[kind, unit].astype(jnp.float32)).astype(jnp.bfloat16)
            chain_copy(kind, False, unit).start()

    def chain_late(kind, unit):
        for hop in range(2, planes - 1):
            chain_hop(kind, hop, unit)

    def chain_early(kind, unit):
        if planes > 2:
            chain_hop(kind, 1, unit)

    def chain_ready(kind, unit):
        if planes == 1:
            return

        @pl.when(lat == 0)
        def _():
            chain_copy(kind, False, unit).wait_recv()

        @pl.when(lat == planes - 1)
        def _():
            chain_copy(kind, True, unit).wait_recv()

    def chain_total(kind, unit):
        ends = up_in[kind, unit].astype(jnp.float32) + down_in[kind, unit].astype(jnp.float32)
        return own[kind, unit].astype(jnp.float32) + ends

    def chain_sent(kind):
        @pl.loop(0, units)
        def _(unit):
            @pl.when(lat < planes - 1)
            def _():
                chain_copy(kind, True, unit).wait_send()

            @pl.when(lat > 0)
            def _():
                chain_copy(kind, False, unit).wait_send()

    def sub_rows(step):
        return pl.ds(pl.multiple_of(step * BLOCK, BLOCK), BLOCK)

    barrier = pltpu.get_barrier_semaphore()
    for k in range(1, lon_count):
        pl.semaphore_signal(
            barrier, inc=1, device_id=(lat, lax.rem(lon + k, lon_count)), device_id_type=pl.DeviceIdType.MESH
        )
    for k in range(1, planes):
        pl.semaphore_signal(
            barrier, inc=1, device_id=(lax.rem(lat + k, planes), lon), device_id_type=pl.DeviceIdType.MESH
        )
    tabs[lon, groups[0]] = lw_ref[...]
    tabs[lon, groups[1]] = sw_ref[...]
    scale_in[lat, pl.ds(0, lw_count)] = lw_scale[...]
    scale_in[lat, pl.ds(lw_count, band_count - lw_count)] = sw_scale[...] * sun_ref[...].astype(jnp.float32)
    scale_in[lat, pl.ds(band_count, scale_in.shape[1] - band_count)] = jnp.zeros(
        (scale_in.shape[1] - band_count, row_count), jnp.float32
    )
    span = pl.ds(pl.multiple_of(lat * part, part), part)
    back_in[lat] = back_ref[:, span]
    back_share[lat] = back_w[:, span]
    coarse_in[lat] = coarse_ref[...]
    share_in[lat] = coarse_w[...]
    stacked[:, pl.ds(0, width)] = cot_ref[...]
    for v in range(var_count):
        stacked[:, pl.ds((v + 1) * width, width)] = inc_ref[v]

    @pl.when(lat == 0)
    def _():
        up_in[...] = jnp.zeros_like(up_in)

    @pl.when(lat == planes - 1)
    def _():
        down_in[...] = jnp.zeros_like(down_in)

    pl.semaphore_wait(barrier, lon_count + planes - 2)
    table_start(0)
    for kinds in ((0, 1), (2, 3, 4)):
        for k in range(1, planes):
            for kind in kinds:
                meta_copy(kind, lax.rem(lat + k, planes), lat).start()

    @pl.loop(0, planes)
    def _(block):
        rows = pl.ds(pl.multiple_of(block * part, part), part)
        table = pick(column_of(perm_ref[:, rows]) == lane_iota(part, col_count))
        moved = dot(table, stacked[...]).astype(jnp.bfloat16)
        cot_out[block] = moved[:, :width].reshape(lon_count, segment, width)
        fields_out[block] = moved[:, width:].reshape(lon_count, segment, flat_width)
        start_block(0, cot_out, cot_in, block)

    table_relay(0)
    table_start(1)
    start_block(1, fields_out, fields_in, 0)

    wait_meta((0, 1))

    @pl.loop(0, planes)
    def _(block):
        spot = lane_iota(part, row_count)
        first, second = column_of(back_in[block, 0:1, :]), column_of(back_in[block, 1:2, :])
        btab[block] = blend(first == spot, second == spot, column_of(back_share[block]))

    @pl.loop(0, planes)
    def _(block):
        wait_block(0, cot_in, block)
        partial = dot(jnp.transpose(cot_in[block].reshape(part, width)), btab[block])
        for step in range(row_blocks):
            own[0, block * row_blocks + step] = partial[:, step * BLOCK : (step + 1) * BLOCK].astype(own.dtype)
            chain_begin(0, block * row_blocks + step)

    def build(group):
        depth = lw_ref.shape[2]
        for b in range(lw_count) if group == 0 else range(lw_count, band_count):
            for v in range(var_count):
                piece = tabs[:, b, v].reshape(lon_count * depth, width)
                wide[pl.ds(v * lon_count * depth, lon_count * depth), pl.ds(b * width, width)] = piece
                turned[pl.ds(b * width, width), pl.ds(v * lon_count * depth, lon_count * depth)] = jnp.transpose(piece)

    table_finish(0)

    table_relay(1)

    @pl.loop(1, planes)
    def _(block):
        start_block(1, fields_out, fields_in, block)

    table_wait(0)
    build(0)

    @pl.loop(0, row_blocks)
    def _(unit):
        chain_early(0, unit)

    table_finish(1)
    table_wait(1)

    build(1)

    wait_meta((2, 3, 4))

    @pl.loop(0, planes + 3)
    def _(turn):
        @pl.when(turn < planes)
        def _():
            block = turn
            wait_block(1, fields_in, block)
            fields_t[...] = jnp.transpose(fields_in[block].reshape(part, flat_width))

            @pl.loop(0, row_blocks)
            def _(step):
                unit = block * row_blocks + step
                rows = sub_rows(step)
                spot = row_iota(part, BLOCK, lat * part)
                index = coarse_in[block, :, rows]
                table = blend(index[0:1, :] == spot, index[1:2, :] == spot, share_in[block, :, rows])
                ctab[block, :, rows] = table
                coarse = dot(fields_t[...], table).astype(jnp.bfloat16)
                scale = scale_in[block, :, rows]
                total = jnp.zeros((width, BLOCK), jnp.float32)
                for start in range(0, band_count, BUNCH):
                    stop = min(start + BUNCH, band_count)
                    bunch = dot(turned[start * width : stop * width, :], coarse)
                    for b in range(start, stop):
                        total = total + scale[b : b + 1, :] * bunch[(b - start) * width : (b - start + 1) * width, :]
                own[1, unit] = total.astype(own.dtype)
                chain_begin(1, unit)
                chain_early(0, unit + row_blocks)
                chain_late(0, unit)
                chain_late(1, unit - 2 * row_blocks)

        @pl.when(turn >= 3)
        def _():
            block = turn - 3
            for step in range(row_blocks):
                unit = block * row_blocks + step
                chain_ready(1, unit)
                heat[pl.ds(step * BLOCK, BLOCK), :] = jnp.transpose(chain_total(1, unit)).astype(jnp.bfloat16)
            moved = dot(btab[block], heat[...]).astype(jnp.bfloat16)
            tend_out[block] = moved.reshape(lon_count, segment, width)
            start_block(3, tend_out, result_in.at[:, :, :, pl.ds(0, width)], block)

        @pl.when((turn >= 1) & (turn <= planes))
        def _():
            block = turn - 1

            @pl.loop(0, row_blocks)
            def _(step):
                unit = block * row_blocks + step
                chain_ready(0, unit)
                rows = sub_rows(step)
                coarse = chain_total(0, unit)
                scale = scale_in[block, :, rows]
                lifted = jnp.concatenate(
                    [(scale[b : b + 1, :] * coarse).astype(jnp.bfloat16) for b in range(band_count)], axis=0
                )
                adj[:, rows] = dot(wide[...], lifted).astype(jnp.bfloat16)
                if planes > 2:

                    @pl.when(block == 0)
                    def _():
                        chain_hop(1, 1, unit)

                    chain_hop(1, 1, unit + row_blocks)

                    @pl.when(block >= planes - 2)
                    def _():
                        chain_late(1, unit)

            moved = lax.dot_general(ctab[block], adj[...], (((1,), (1,)), ((), ())), preferred_element_type=jnp.float32)
            grad_out[block] = moved.astype(jnp.bfloat16).reshape(lon_count, segment, flat_width)
            start_block(2, grad_out, result_in.at[:, :, :, pl.ds(width, flat_width)], block)

    for group in range(2):
        table_sent(group)

    @pl.loop(1, planes)
    def _(k):
        for kind in range(5):
            meta_copy(kind, lax.rem(lat + k, planes), lat).wait_send()

    chain_sent(0)
    chain_sent(1)
    wait_sent(0, cot_out)
    wait_sent(1, fields_out)

    @pl.loop(0, planes)
    def _(block):
        wait_block(2, result_in.at[:, :, :, pl.ds(width, flat_width)], block)
        wait_block(3, result_in.at[:, :, :, pl.ds(0, width)], block)

    wait_sent(2, grad_out)
    wait_sent(3, tend_out)


def restore_kernel(perm_ref, result_ref, tend_done, grad_done):
    rows, width = tend_done.shape
    col_count = result_ref.shape[0]
    table = pick(perm_ref[...] == row_iota(rows, col_count, pl.program_id(0) * rows))
    moved = dot(table, result_ref[...]).astype(jnp.bfloat16)
    tend_done[...] = moved[:, :width]
    for v in range(grad_done.shape[0]):
        grad_done[v] = moved[:, (v + 1) * width : (v + 2) * width]


def local(
    increments,
    cotangent,
    owner_perm,
    coarse_index,
    coarse_weight,
    back_index,
    back_weight,
    lw_scale,
    sw_scale,
    sunlit,
    lw_table,
    sw_table,
    *,
    planes,
    lon_count,
):
    col_count, var_count, width = increments.shape
    row_count = coarse_weight.shape[0]
    segment = col_count // (planes * lon_count)
    part = lon_count * segment
    flat_width = var_count * width
    thin, thick = (planes, lon_count, segment, width), (planes, lon_count, segment, flat_width)
    bands = lw_table.shape[0] + sw_table.shape[0]
    scale_rows = -(-(bands + 1) // 8) * 8
    wire = (2, planes * (row_count // BLOCK), width, BLOCK)
    half, full, whole = jnp.bfloat16, jnp.float32, jnp.int32
    vmem = pl.BlockSpec(memory_space=pltpu.VMEM)
    scratch = [
        ((col_count, (var_count + 1) * width), half),
        (thin, half),
        (thin, half),
        (thick, half),
        (thick, half),
        (thick, half),
        (thin, half),
        ((lon_count, bands) + lw_table.shape[1:], half),
        ((flat_width, bands * width), half),
        ((bands * width, flat_width), half),
        ((planes, part, row_count), half),
        ((planes, part, row_count), half),
        ((flat_width, part), half),
        ((flat_width, row_count), half),
        ((row_count, width), half),
        (wire, half),
        (wire, half),
        (wire, half),
        (wire, half),
        (wire, full if planes * row_count <= WIDE_SUMS else half),
        ((planes, scale_rows, row_count), full),
        ((planes, 2, row_count), whole),
        ((planes, 1, row_count), full),
        ((planes, 2, part), whole),
        ((planes, 1, part), full),
    ]
    units = planes * (row_count // BLOCK)
    sems = (
        (4, planes, lon_count),
        (4, planes, lon_count),
        (2, 2, units),
        (2, 2, units),
        (5, planes),
        (5, planes),
        (2, lon_count // 2 + 2, lon_count),
        (2, lon_count),
    )
    stack_width = (var_count + 1) * width
    args = (
        owner_perm,
        jnp.transpose(increments, (1, 0, 2)),
        cotangent,
        back_index,
        back_weight[None, :],
        lw_scale,
        sw_scale,
        sunlit[None, :],
        lw_table,
        sw_table,
        coarse_index,
        coarse_weight[None, :],
    )
    received = pl.pallas_call(
        radiate_kernel,
        out_shape=jax.ShapeDtypeStruct((planes, lon_count, segment, stack_width), half),
        in_specs=[vmem] * len(args),
        out_specs=vmem,
        scratch_shapes=[pltpu.VMEM(shape, kind) for shape, kind in scratch]
        + [pltpu.SemaphoreType.DMA(shape) for shape in sems],
        compiler_params=pltpu.CompilerParams(
            vmem_limit_bytes=62 * 1024 * 1024, has_side_effects=True, collective_id=0
        ),
        cost_estimate=pl.CostEstimate(
            flops=12 * planes * row_count * bands * flat_width * width, bytes_accessed=4 << 20, transcendentals=0
        ),
    )(*args)
    steps = col_count // FINAL
    tendency, gradient = pl.pallas_call(
        restore_kernel,
        grid=(steps,),
        out_shape=[
            jax.ShapeDtypeStruct((col_count, width), half),
            jax.ShapeDtypeStruct((var_count, col_count, width), half),
        ],
        in_specs=[
            pl.BlockSpec((1, col_count), lambda i: (0, 0)),
            pl.BlockSpec((col_count, stack_width), lambda i: (0, 0)),
        ],
        out_specs=[
            pl.BlockSpec((FINAL, width), lambda i: (i, 0)),
            pl.BlockSpec((var_count, FINAL, width), lambda i: (0, i, 0)),
        ],
        compiler_params=pltpu.CompilerParams(vmem_limit_bytes=32 * 1024 * 1024),
        cost_estimate=pl.CostEstimate(
            flops=2 * col_count * col_count * stack_width, bytes_accessed=4 << 20, transcendentals=0
        ),
    )(owner_perm, received.reshape(col_count, stack_width))
    return (tendency, jnp.transpose(gradient, (1, 0, 2)))


def solution(mesh):
    in_specs = (
        P(("lat", "lon"), None, None),
        P(("lat", "lon"), None),
        P(("lat", "lon"), None),
        P(None, ("lat", "lon")),
        P(("lat", "lon")),
        P(None, ("lat", "lon")),
        P(("lat", "lon")),
        P(None, ("lat", "lon")),
        P(None, ("lat", "lon")),
        P(("lat", "lon")),
        P(None, None, "lon", None),
        P(None, None, "lon", None),
    )
    out_specs = (P(("lat", "lon"), None), P(("lat", "lon"), None, None))

    def body(*args):
        return local(*args, planes=mesh.shape["lat"], lon_count=mesh.shape["lon"])

    return jax.shard_map(body, mesh=mesh, in_specs=in_specs, out_specs=out_specs, check_vma=False)
```

time: 140 us -> 113 us (0.81)
  Pallas kernels: 135 us -> 111 us
  local copies, waits for them, and re-layouts: 4.52 us -> 1.59 us
    pallas_call x1 -> x2, Pallas kernels: 135 us -> 111 us  [the longest x1 105 us: local(): pl.pallas_call(radiate_kernel, out_shape=jax.ShapeDtypeStruct((planes, lo...]
    unnamed x2 -> x4, local copies, waits for them, and re-layouts: 4.52 us -> 1.59 us
where the time goes in v2:
time: 113 us
  Pallas kernels  111 us (98%)
  local copies, waits for them, and re-layouts  1.59 us (1%)
    pallas_call x1, Pallas kernels, local(): pl.pallas_call(radiate_kernel, out_shape=jax.ShapeDtypeStruct((planes, lo...  105 us
    pallas_call x1, Pallas kernels, local(): pl.pallas_call(restore_kernel, grid=(steps,), out_shape=[jax.ShapeDtypeSt...  5.82 us

profile of v2, /device:TPU:0, one launch (start us, length us, event | category | flops | bytes accessed | tf_op | source)
XLA Modules:
  0.0 112.8 jit_solution(9487577473607533931)
XLA Ops:
  0.6 0.0 copy-start
  0.6 104.7 %shard_map.131 = bf16[4,8,64,512]{3,2,1,0:T(8,128)(2,1)} custom-call(s32[1,2048]{1,0:T(1,128)} %perm_ref.3, bf16[3,2048,128]{2,1,0:T(8,128)(2,1)} %bitcast.7, bf16[2048,128]{1,0:T(8,128)(2,1)} %cot_ref.1, s32[2,2048]{1,0:T(2,128)} %back_ref.1, f32[1,2048]{1,0:T(1,128)} %bitcast.8, f32[16,1024]{1,0:T(8,128)} %lw_scale.1, f32[14,1024]{1,0:T(8,128)} %sw_scale.1, ...), custom_call_target="tpu_custom_call" | custom-call | flops 72477573120 | bytes 4194304 | tf_op jit(solution)/shard_map/pallas_call | solution.py:565
  105.4 0.0 copy-done
  105.4 0.0 copy-start.1
  105.4 1.6 %copy-done.1 = bf16[4,8,64,512]{3,2,1,0:T(8,128)(2,1)S(1)} copy-done((bf16[4,8,64,512]{3,2,1,0:T(8,128)(2,1)S(1)}, bf16[4,8,64,512]{3,2,1,0:T(8,128)(2,1)}, u32[]{:S(2)}) %copy-start.1) | copy-done | bytes 2097176
  107.0 5.8 %shard_map.132 = (bf16[2048,128]{1,0:T(8,128)(2,1)}, bf16[3,2048,128]{2,1,0:T(8,128)(2,1)}) custom-call(s32[1,2048]{1,0:T(1,128)S(1)} %copy-done, bf16[2048,512]{1,0:T(8,128)(2,1)S(1)} %bitcast.6), custom_call_target="tpu_custom_call" | custom-call | flops 4294967296 | bytes 4194304 | tf_op jit(solution)/shard_map/pallas_call | solution.py:580
Async XLA Ops:
  0.6 104.8 %copy-start = (s32[1,2048]{1,0:T(1,128)S(1)}, s32[1,2048]{1,0:T(1,128)}, u32[]{:S(2)}) copy-start(s32[1,2048]{1,0:T(1,128)} %perm_ref.3) | copy-start | bytes 24580
  105.4 1.6 %copy-start.1 = (bf16[4,8,64,512]{3,2,1,0:T(8,128)(2,1)S(1)}, bf16[4,8,64,512]{3,2,1,0:T(8,128)(2,1)}, u32[]{:S(2)}) copy-start(bf16[4,8,64,512]{3,2,1,0:T(8,128)(2,1)} %shard_map.131) | copy-start | bytes 6291460

commit v3 on v2

--- a/solution.py
+++ b/solution.py
@@ -64,6 +64,7 @@
     ctab,
     btab,
     fields_t,
+    kept,
     adj,
     heat,
     up_out,
@@ -84,6 +85,7 @@
     meta_recv,
     tab_send,
     tab_recv,
+    keep_sem,
 ):
     var_count, col_count, width = inc_ref.shape
     planes, lon_count, segment = cot_out.shape[0], cot_out.shape[1], cot_out.shape[2]
@@ -97,7 +99,9 @@
     lat, lon = lax.axis_index("lat"), lax.axis_index("lon")
     parity = lax.rem(lon, 2)
     partner = lon + 1 - 2 * parity
-    groups = (pl.ds(0, lw_count), pl.ds(lw_count, band_count - lw_count))
+    lw_half, sw_half = lw_count // 2, lw_count + (band_count - lw_count) // 2
+    edges = (0, lw_half, lw_count, sw_half, band_count)
+    groups = tuple(pl.ds(edges[i], edges[i + 1] - edges[i]) for i in range(4))
 
     def remote(source, landing, send, recv, target_lat, target_lon):
         return pltpu.make_async_remote_copy(
@@ -109,9 +113,9 @@
             device_id_type=pl.DeviceIdType.MESH,
         )
 
-    def table_copy(group, slot, target, hop):
+    def table_copy(group, slot, target):
         piece = tabs.at[slot, groups[group]]
-        return remote(piece, piece, tab_send.at[group, hop, target], tab_recv.at[group, slot], lat, target)
+        return remote(piece, piece, tab_send.at[group], tab_recv.at[group, slot], lat, target)
 
     quad = lon_count == 8
     if quad:
@@ -121,73 +125,63 @@
     else:
         near, far = tuple(lax.rem(lon + 2 * j, lon_count) for j in range(1, lon_count // 2)), None
 
-    def relay(group, done):
-        @pl.when(parity == 0)
-        def _():
-            piece = table_copy(group, near[0], near[1], 1)
-            piece.wait_send() if done else piece.start()
-
-        @pl.when(parity == 1)
-        def _():
-            piece = table_copy(group, near[1], near[0], 1)
-            piece.wait_send() if done else piece.start()
-
-    def table_start(group):
-        for target in near + (partner,):
-            table_copy(group, lon, target, 0).start()
-
-    def table_relay(group):
-        for source in near:
-            table_copy(group, source, source, 0).wait_recv()
+    def relay(group):
+        return table_copy(group, near[group % 2], near[1 - group % 2])
+
+    def table_start(half):
+        for group in (2 * half, 2 * half + 1):
+            for target in near + (partner,):
+                table_copy(group, lon, target).start()
+
+    def table_relay(half):
+        for group in (2 * half, 2 * half + 1):
+            for source in near:
+                table_copy(group, source, source).wait_recv()
+            if quad:
+                relay(group).start()
+            for source in near:
+                table_copy(group, source, partner).start()
+
+    def table_finish(half):
         if quad:
-            relay(group, False)
-        for j, source in enumerate(near):
-            table_copy(group, source, partner, 2 + j).start()
-
-    def table_finish(group):
-        if quad:
-            table_copy(group, far, far, 0).wait_recv()
-            table_copy(group, far, partner, 2 + len(near)).start()
-
-    def table_wait(group):
-        for j in range(lon_count // 2):
-            source = lax.rem(partner + 2 * j, lon_count)
-            table_copy(group, source, source, 0).wait_recv()
+            for group in (2 * half, 2 * half + 1):
+                table_copy(group, far, far).wait_recv()
+                table_copy(group, far, partner).start()
+
+    def table_wait(half):
+        for group in (2 * half, 2 * half + 1):
+            for j in range(lon_count // 2):
+                source = lax.rem(partner + 2 * j, lon_count)
+                table_copy(group, source, source).wait_recv()
 
     def table_sent(group):
-        for target in near + (partner,):
-            table_copy(group, lon, target, 0).wait_send()
-        if quad:
-            relay(group, True)
-        for j, source in enumerate(near + ((far,) if quad else ())):
-            table_copy(group, source, partner, 2 + j).wait_send()
-
-    def copy(kind, source, landing, block, target, slot):
-        return remote(source, landing, send_sem.at[kind, block, target], recv_sem.at[kind, block, slot], lat, target)
+        pieces = tabs.at[pl.ds(0, lon_count - 1), groups[group]]
+        remote(pieces, pieces, tab_send.at[group], tab_recv.at[group, 0], lat, partner).wait_send()
+
+    def copy(kind, source, landing, block, target):
+        return remote(source, landing, send_sem.at[kind], recv_sem.at[kind, block], lat, target)
+
+    def keep_copy(kind, source, landing, block):
+        return pltpu.make_async_copy(source.at[block, lon], landing.at[block, lon], keep_sem.at[kind - 2])
 
     def start_block(kind, source, landing, block):
-        landing.at[block, lon][...] = source[block, lon]
+        if kind < 2:
+            landing[block, lon] = source[block, lon]
+        else:
+            keep_copy(kind, source, landing, block).start()
 
         @pl.loop(1, lon_count)
         def _(k):
             target = lax.rem(lon + k, lon_count)
-            copy(kind, source.at[block, target], landing.at[block, lon], block, target, lon).start()
+            copy(kind, source.at[block, target], landing.at[block, lon], block, target).start()
 
     def wait_block(kind, landing, block):
-        @pl.loop(1, lon_count)
-        def _(k):
-            source = lax.rem(lon + k, lon_count)
-            piece = landing.at[block, source]
-            copy(kind, piece, piece, block, source, source).wait_recv()
+        pieces = landing.at[block, pl.ds(0, lon_count - 1)]
+        copy(kind, pieces, pieces, block, partner).wait_recv()
 
     def wait_sent(kind, source):
-        @pl.loop(0, planes)
-        def _(block):
-            @pl.loop(1, lon_count)
-            def _(k):
-                target = lax.rem(lon + k, lon_count)
-                piece = source.at[block, target]
-                copy(kind, piece, piece, block, target, target).wait_send()
+        pieces = source.at[:, pl.ds(0, lon_count - 1)]
+        copy(kind, pieces, pieces, 0, partner).wait_send()
 
     def meta_copy(kind, target, slot):
         span = pl.ds(pl.multiple_of(target * part, part), part)
@@ -198,20 +192,22 @@
             (coarse_w, share_in.at[slot]),
             (scale_in.at[slot], scale_in.at[slot]),
         )[kind]
-        return remote(source, landing, meta_send.at[kind, target], meta_recv.at[kind, slot], target, lon)
+        return remote(source, landing, meta_send.at[kind], meta_recv.at[kind], target, lon)
+
+    def meta_whole(kind):
+        pieces = (back_in, back_share, coarse_in, share_in, scale_in)[kind].at[pl.ds(0, planes - 1)]
+        return remote(pieces, pieces, meta_send.at[kind], meta_recv.at[kind], lat, partner)
 
     def wait_meta(kinds):
-        @pl.loop(1, planes)
-        def _(k):
-            source = lax.rem(lat + k, planes)
+        if planes > 1:
             for kind in kinds:
-                meta_copy(kind, source, source).wait_recv()
+                meta_whole(kind).wait_recv()
 
     def chain_copy(kind, upward, unit):
         out, landing, way = (up_out, up_in, 0) if upward else (down_out, down_in, 1)
         target = lat + 1 if upward else lat - 1
         piece, spot = out.at[kind, unit], landing.at[kind, unit]
-        return remote(piece, spot, chain_send.at[kind, way, unit], chain_recv.at[kind, way, unit], target, lon)
+        return remote(piece, spot, chain_send.at[kind, way], chain_recv.at[kind, way, unit], target, lon)
 
     def chain_begin(kind, unit):
         if planes == 1:
@@ -265,15 +261,15 @@
         return own[kind, unit].astype(jnp.float32) + ends
 
     def chain_sent(kind):
-        @pl.loop(0, units)
-        def _(unit):
-            @pl.when(lat < planes - 1)
-            def _():
-                chain_copy(kind, True, unit).wait_send()
-
-            @pl.when(lat > 0)
-            def _():
-                chain_copy(kind, False, unit).wait_send()
+        @pl.when(lat < planes - 1)
+        def _():
+            pieces = up_out.at[kind]
+            remote(pieces, pieces, chain_send.at[kind, 0], chain_recv.at[kind, 0, 0], lat, partner).wait_send()
+
+        @pl.when(lat > 0)
+        def _():
+            pieces = down_out.at[kind]
+            remote(pieces, pieces, chain_send.at[kind, 1], chain_recv.at[kind, 1, 0], lat, partner).wait_send()
 
     def sub_rows(step):
         return pl.ds(pl.multiple_of(step * BLOCK, BLOCK), BLOCK)
@@ -287,8 +283,8 @@
         pl.semaphore_signal(
             barrier, inc=1, device_id=(lax.rem(lat + k, planes), lon), device_id_type=pl.DeviceIdType.MESH
         )
-    tabs[lon, groups[0]] = lw_ref[...]
-    tabs[lon, groups[1]] = sw_ref[...]
+    tabs[lon, pl.ds(0, lw_count)] = lw_ref[...]
+    tabs[lon, pl.ds(lw_count, band_count - lw_count)] = sw_ref[...]
     scale_in[lat, pl.ds(0, lw_count)] = lw_scale[...]
     scale_in[lat, pl.ds(lw_count, band_count - lw_count)] = sw_scale[...] * sun_ref[...].astype(jnp.float32)
     scale_in[lat, pl.ds(band_count, scale_in.shape[1] - band_count)] = jnp.zeros(
@@ -328,8 +324,8 @@
         start_block(0, cot_out, cot_in, block)
 
     table_relay(0)
+    start_block(1, fields_out, fields_in, 0)
     table_start(1)
-    start_block(1, fields_out, fields_in, 0)
 
     wait_meta((0, 1))
 
@@ -355,7 +351,41 @@
                 wide[pl.ds(v * lon_count * depth, lon_count * depth), pl.ds(b * width, width)] = piece
                 turned[pl.ds(b * width, width), pl.ds(v * lon_count * depth, lon_count * depth)] = jnp.transpose(piece)
 
+    def bands(first, last, block, rows, coarse, total):
+        scale = scale_in[block, :, rows]
+        for start in range(first, last, BUNCH):
+            stop = min(start + BUNCH, last)
+            bunch = dot(turned[start * width : stop * width, :], coarse)
+            for b in range(start, stop):
+                total = total + scale[b : b + 1, :] * bunch[(b - start) * width : (b - start + 1) * width, :]
+        return total
+
+    def gather_fields(block):
+        wait_block(1, fields_in, block)
+        fields_t[...] = jnp.transpose(fields_in[block].reshape(part, flat_width))
+
+    def interpolate(block, rows):
+        spot = row_iota(part, BLOCK, lat * part)
+        index = coarse_in[block, :, rows]
+        table = blend(index[0:1, :] == spot, index[1:2, :] == spot, share_in[block, :, rows])
+        ctab[block, :, rows] = table
+        return dot(fields_t[...], table).astype(jnp.bfloat16)
+
     table_finish(0)
+    table_wait(0)
+
+    build(0)
+    wait_meta((2, 3, 4))
+
+    gather_fields(0)
+
+    @pl.loop(0, row_blocks)
+    def _(step):
+        rows = sub_rows(step)
+        coarse = interpolate(0, rows)
+        kept[step] = coarse
+        own[1, step] = bands(0, lw_count, 0, rows, coarse, jnp.zeros((width, BLOCK), jnp.float32)).astype(own.dtype)
+        chain_early(0, step)
 
     table_relay(1)
 
@@ -363,64 +393,66 @@
     def _(block):
         start_block(1, fields_out, fields_in, block)
 
-    table_wait(0)
-    build(0)
-
     @pl.loop(0, row_blocks)
-    def _(unit):
-        chain_early(0, unit)
+    def _(step):
+        chain_early(0, step + row_blocks)
+        chain_late(0, step)
 
     table_finish(1)
     table_wait(1)
 
     build(1)
 
-    wait_meta((2, 3, 4))
-
-    @pl.loop(0, planes + 3)
+    @pl.loop(0, planes)
     def _(turn):
-        @pl.when(turn < planes)
+        def follow(unit):
+            chain_begin(1, unit)
+            chain_early(0, unit + 2 * row_blocks)
+            chain_late(0, unit + row_blocks)
+            chain_early(1, unit - 2 * row_blocks)
+            chain_late(1, unit - 3 * row_blocks)
+
+        @pl.when(turn == 0)
+        def _():
+            @pl.loop(0, row_blocks)
+            def _(step):
+                begun = own[1, step].astype(jnp.float32)
+                total = bands(lw_count, band_count, 0, sub_rows(step), kept[step], begun)
+                own[1, step] = total.astype(own.dtype)
+                follow(step)
+
+        @pl.when(turn > 0)
         def _():
             block = turn
-            wait_block(1, fields_in, block)
-            fields_t[...] = jnp.transpose(fields_in[block].reshape(part, flat_width))
+            gather_fields(block)
 
             @pl.loop(0, row_blocks)
             def _(step):
                 unit = block * row_blocks + step
                 rows = sub_rows(step)
-                spot = row_iota(part, BLOCK, lat * part)
-                index = coarse_in[block, :, rows]
-                table = blend(index[0:1, :] == spot, index[1:2, :] == spot, share_in[block, :, rows])
-                ctab[block, :, rows] = table
-                coarse = dot(fields_t[...], table).astype(jnp.bfloat16)
-                scale = scale_in[block, :, rows]
-                total = jnp.zeros((width, BLOCK), jnp.float32)
-                for start in range(0, band_count, BUNCH):
-                    stop = min(start + BUNCH, band_count)
-                    bunch = dot(turned[start * width : stop * width, :], coarse)
-                    for b in range(start, stop):
-                        total = total + scale[b : b + 1, :] * bunch[(b - start) * width : (b - start + 1) * width, :]
-                own[1, unit] = total.astype(own.dtype)
-                chain_begin(1, unit)
-                chain_early(0, unit + row_blocks)
-                chain_late(0, unit)
-                chain_late(1, unit - 2 * row_blocks)
-
-        @pl.when(turn >= 3)
-        def _():
-            block = turn - 3
-            for step in range(row_blocks):
-                unit = block * row_blocks + step
-                chain_ready(1, unit)
-                heat[pl.ds(step * BLOCK, BLOCK), :] = jnp.transpose(chain_total(1, unit)).astype(jnp.bfloat16)
-            moved = dot(btab[block], heat[...]).astype(jnp.bfloat16)
-            tend_out[block] = moved.reshape(lon_count, segment, width)
-            start_block(3, tend_out, result_in.at[:, :, :, pl.ds(0, width)], block)
-
-        @pl.when((turn >= 1) & (turn <= planes))
-        def _():
-            block = turn - 1
+                coarse = interpolate(block, rows)
+                zero = jnp.zeros((width, BLOCK), jnp.float32)
+                own[1, unit] = bands(0, band_count, block, rows, coarse, zero).astype(own.dtype)
+                follow(unit)
+
+    def finish_heat(block):
+        for step in range(row_blocks):
+            unit = block * row_blocks + step
+            chain_ready(1, unit)
+            heat[pl.ds(step * BLOCK, BLOCK), :] = jnp.transpose(chain_total(1, unit)).astype(jnp.bfloat16)
+        moved = dot(btab[block], heat[...]).astype(jnp.bfloat16)
+        tend_out[block] = moved.reshape(lon_count, segment, width)
+        start_block(3, tend_out, result_in.at[:, :, :, pl.ds(0, width)], block)
+
+    @pl.loop(0, planes + 1)
+    def _(turn):
+        @pl.when(turn > 0)
+        def _():
+            finish_heat(turn - 1)
+
+        @pl.when(turn < planes)
+        def _():
+            block = turn
 
             @pl.loop(0, row_blocks)
             def _(step):
@@ -433,29 +465,19 @@
                     [(scale[b : b + 1, :] * coarse).astype(jnp.bfloat16) for b in range(band_count)], axis=0
                 )
                 adj[:, rows] = dot(wide[...], lifted).astype(jnp.bfloat16)
-                if planes > 2:
-
-                    @pl.when(block == 0)
-                    def _():
-                        chain_hop(1, 1, unit)
-
-                    chain_hop(1, 1, unit + row_blocks)
-
-                    @pl.when(block >= planes - 2)
-                    def _():
-                        chain_late(1, unit)
+                chain_early(1, unit + units - 2 * row_blocks)
+                chain_late(1, unit + units - 3 * row_blocks)
 
             moved = lax.dot_general(ctab[block], adj[...], (((1,), (1,)), ((), ())), preferred_element_type=jnp.float32)
             grad_out[block] = moved.astype(jnp.bfloat16).reshape(lon_count, segment, flat_width)
             start_block(2, grad_out, result_in.at[:, :, :, pl.ds(width, flat_width)], block)
 
-    for group in range(2):
+    for group in range(4):
         table_sent(group)
 
-    @pl.loop(1, planes)
-    def _(k):
+    if planes > 1:
         for kind in range(5):
-            meta_copy(kind, lax.rem(lat + k, planes), lat).wait_send()
+            meta_whole(kind).wait_send()
 
     chain_sent(0)
     chain_sent(1)
@@ -469,6 +491,11 @@
 
     wait_sent(2, grad_out)
     wait_sent(3, tend_out)
+
+    for kind, source, start in ((2, grad_out, width), (3, tend_out, 0)):
+        piece = source.at[:, 0]
+        kept_piece = result_in.at[:, 0, :, pl.ds(start, source.shape[-1])]
+        pltpu.make_async_copy(piece, kept_piece, keep_sem.at[kind - 2]).wait()
 
 
 def restore_kernel(perm_ref, result_ref, tend_done, grad_done):
@@ -523,6 +550,7 @@
         ((planes, part, row_count), half),
         ((planes, part, row_count), half),
         ((flat_width, part), half),
+        ((row_count // BLOCK, flat_width, BLOCK), half),
         ((flat_width, row_count), half),
         ((row_count, width), half),
         (wire, half),
@@ -538,14 +566,15 @@
     ]
     units = planes * (row_count // BLOCK)
     sems = (
-        (4, planes, lon_count),
-        (4, planes, lon_count),
+        (4,),
+        (4, planes),
+        (2, 2),
         (2, 2, units),
-        (2, 2, units),
-        (5, planes),
-        (5, planes),
-        (2, lon_count // 2 + 2, lon_count),
-        (2, lon_count),
+        (5,),
+        (5,),
+        (4,),
+        (4, lon_count),
+        (2,),
     )
     stack_width = (var_count + 1) * width
     args = (
@@ -566,7 +595,7 @@
         radiate_kernel,
         out_shape=jax.ShapeDtypeStruct((planes, lon_count, segment, stack_width), half),
         in_specs=[vmem] * len(args),
-        out_specs=vmem,
+        out_specs=pl.BlockSpec(memory_space=pl.ANY),
         scratch_shapes=[pltpu.VMEM(shape, kind) for shape, kind in scratch]
         + [pltpu.SemaphoreType.DMA(shape) for shape in sems],
         compiler_params=pltpu.CompilerParams(

time: 113 us -> 97.2 us (0.86)
  Pallas kernels: 111 us -> 94.8 us
    pallas_call x1, Pallas kernels: 105 us -> 88.9 us  [local(): pl.pallas_call(radiate_kernel, out_shape=jax.ShapeDtypeStruct((planes, lo...]
where the time goes in v3:
time: 97.2 us; the launch traced here: 97 us
  Pallas kernels  94.8 us (98%)
  local copies, waits for them, and re-layouts  1.59 us (2%)
    pallas_call x1, Pallas kernels, local(): pl.pallas_call(radiate_kernel, out_shape=jax.ShapeDtypeStruct((planes, lo...  88.9 us
    pallas_call x1, Pallas kernels, local(): pl.pallas_call(restore_kernel, grid=(steps,), out_shape=[jax.ShapeDtypeSt...  5.82 us

profile of v3, /device:TPU:0, one launch (start us, length us, event | category | flops | bytes accessed | tf_op | source)
XLA Modules:
  0.0 97.0 jit_solution(2669189131925808000)
XLA Ops:
  0.6 0.0 copy-start
  0.6 88.9 %shard_map.131 = bf16[4,8,64,512]{3,2,1,0:T(8,128)(2,1)} custom-call(s32[1,2048]{1,0:T(1,128)} %perm_ref.3, bf16[3,2048,128]{2,1,0:T(8,128)(2,1)} %bitcast.7, bf16[2048,128]{1,0:T(8,128)(2,1)} %cot_ref.1, s32[2,2048]{1,0:T(2,128)} %back_ref.1, f32[1,2048]{1,0:T(1,128)} %bitcast.8, f32[16,1024]{1,0:T(8,128)} %lw_scale.1, f32[14,1024]{1,0:T(8,128)} %sw_scale.1, ...), custom_call_target="tpu_custom_call" | custom-call | flops 72477573120 | bytes 4194304 | tf_op jit(solution)/shard_map/pallas_call | solution.py:594
  89.6 0.0 copy-done
  89.6 0.0 copy-start.1
  89.6 1.6 %copy-done.1 = bf16[4,8,64,512]{3,2,1,0:T(8,128)(2,1)S(1)} copy-done((bf16[4,8,64,512]{3,2,1,0:T(8,128)(2,1)S(1)}, bf16[4,8,64,512]{3,2,1,0:T(8,128)(2,1)}, u32[]{:S(2)}) %copy-start.1) | copy-done | bytes 2097176
  91.2 5.8 %shard_map.132 = (bf16[2048,128]{1,0:T(8,128)(2,1)}, bf16[3,2048,128]{2,1,0:T(8,128)(2,1)}) custom-call(s32[1,2048]{1,0:T(1,128)S(1)} %copy-done, bf16[2048,512]{1,0:T(8,128)(2,1)S(1)} %bitcast.6), custom_call_target="tpu_custom_call" | custom-call | flops 4294967296 | bytes 4194304 | tf_op jit(solution)/shard_map/pallas_call | solution.py:609
Async XLA Ops:
  0.6 89.0 %copy-start = (s32[1,2048]{1,0:T(1,128)S(1)}, s32[1,2048]{1,0:T(1,128)}, u32[]{:S(2)}) copy-start(s32[1,2048]{1,0:T(1,128)} %perm_ref.3) | copy-start | bytes 24580
  89.6 1.6 %copy-start.1 = (bf16[4,8,64,512]{3,2,1,0:T(8,128)(2,1)S(1)}, bf16[4,8,64,512]{3,2,1,0:T(8,128)(2,1)}, u32[]{:S(2)}) copy-start(bf16[4,8,64,512]{3,2,1,0:T(8,128)(2,1)} %shard_map.131) | copy-start | bytes 6291460

commit v4 on v3

--- a/solution.py
+++ b/solution.py
@@ -9,6 +9,7 @@
 FINAL = 512
 BUNCH = 3
 WIDE_SUMS = 4096
+LOADED = (1, 2, 8, 9)
 
 
 def lane_iota(rows, width):
@@ -51,6 +52,9 @@
     coarse_ref,
     coarse_w,
     result_in,
+    restored,
+    early_in,
+    staged,
     stacked,
     cot_out,
     cot_in,
@@ -86,6 +90,8 @@
     tab_send,
     tab_recv,
     keep_sem,
+    load_sem,
+    put_sem,
 ):
     var_count, col_count, width = inc_ref.shape
     planes, lon_count, segment = cot_out.shape[0], cot_out.shape[1], cot_out.shape[2]
@@ -96,6 +102,9 @@
     flat_width = var_count * width
     row_blocks = row_count // BLOCK
     units = planes * row_blocks
+    half = planes // 2
+    early = early_in.shape[0]
+    lanes = (pl.ds(width, flat_width), pl.ds(0, width))
     lat, lon = lax.axis_index("lat"), lax.axis_index("lon")
     parity = lax.rem(lon, 2)
     partner = lon + 1 - 2 * parity
@@ -128,13 +137,13 @@
     def relay(group):
         return table_copy(group, near[group % 2], near[1 - group % 2])
 
-    def table_start(half):
-        for group in (2 * half, 2 * half + 1):
+    def table_start(side):
+        for group in (2 * side, 2 * side + 1):
             for target in near + (partner,):
                 table_copy(group, lon, target).start()
 
-    def table_relay(half):
-        for group in (2 * half, 2 * half + 1):
+    def table_relay(side):
+        for group in (2 * side, 2 * side + 1):
             for source in near:
                 table_copy(group, source, source).wait_recv()
             if quad:
@@ -142,14 +151,14 @@
             for source in near:
                 table_copy(group, source, partner).start()
 
-    def table_finish(half):
+    def table_finish(side):
         if quad:
-            for group in (2 * half, 2 * half + 1):
+            for group in (2 * side, 2 * side + 1):
                 table_copy(group, far, far).wait_recv()
                 table_copy(group, far, partner).start()
 
-    def table_wait(half):
-        for group in (2 * half, 2 * half + 1):
+    def table_wait(side):
+        for group in (2 * side, 2 * side + 1):
             for j in range(lon_count // 2):
                 source = lax.rem(partner + 2 * j, lon_count)
                 table_copy(group, source, source).wait_recv()
@@ -161,19 +170,31 @@
     def copy(kind, source, landing, block, target):
         return remote(source, landing, send_sem.at[kind], recv_sem.at[kind, block], lat, target)
 
-    def keep_copy(kind, source, landing, block):
-        return pltpu.make_async_copy(source.at[block, lon], landing.at[block, lon], keep_sem.at[kind - 2])
-
-    def start_block(kind, source, landing, block):
+    def start_block(kind, source, landing, block, spot=None):
+        spot = block if spot is None else spot
+        landing = landing.at[spot, lon]
         if kind < 2:
-            landing[block, lon] = source[block, lon]
+            landing[...] = source[block, lon]
         else:
-            keep_copy(kind, source, landing, block).start()
+            pltpu.make_async_copy(source.at[block, lon], landing, keep_sem.at[kind - 2]).start()
 
         @pl.loop(1, lon_count)
         def _(k):
             target = lax.rem(lon + k, lon_count)
-            copy(kind, source.at[block, target], landing.at[block, lon], block, target).start()
+            copy(kind, source.at[block, target], landing, block, target).start()
+
+    def return_block(kind, source, block):
+        @pl.when(block < early)
+        def _():
+            start_block(kind, source, early_in.at[:, :, :, lanes[kind - 2]], block)
+
+        @pl.when(block >= early)
+        def _():
+            start_block(kind, source, result_in.at[:, :, :, lanes[kind - 2]], block, block - early)
+
+    def wait_return(block):
+        for kind, landing in ((2, grad_out), (3, tend_out)):
+            wait_block(kind, landing, block)
 
     def wait_block(kind, landing, block):
         pieces = landing.at[block, pl.ds(0, lon_count - 1)]
@@ -283,8 +304,16 @@
         pl.semaphore_signal(
             barrier, inc=1, device_id=(lax.rem(lat + k, planes), lon), device_id_type=pl.DeviceIdType.MESH
         )
-    tabs[lon, pl.ds(0, lw_count)] = lw_ref[...]
-    tabs[lon, pl.ds(lw_count, band_count - lw_count)] = sw_ref[...]
+    loads = [
+        pltpu.make_async_copy(lw_ref, tabs.at[lon, pl.ds(0, lw_count)], load_sem.at[0]),
+        pltpu.make_async_copy(sw_ref, tabs.at[lon, pl.ds(lw_count, band_count - lw_count)], load_sem.at[1]),
+        pltpu.make_async_copy(cot_ref, stacked.at[:, pl.ds(0, width)], load_sem.at[2]),
+    ] + [
+        pltpu.make_async_copy(inc_ref.at[v], stacked.at[:, pl.ds((v + 1) * width, width)], load_sem.at[3 + v])
+        for v in range(var_count)
+    ]
+    for load in loads:
+        load.start()
     scale_in[lat, pl.ds(0, lw_count)] = lw_scale[...]
     scale_in[lat, pl.ds(lw_count, band_count - lw_count)] = sw_scale[...] * sun_ref[...].astype(jnp.float32)
     scale_in[lat, pl.ds(band_count, scale_in.shape[1] - band_count)] = jnp.zeros(
@@ -295,9 +324,6 @@
     back_share[lat] = back_w[:, span]
     coarse_in[lat] = coarse_ref[...]
     share_in[lat] = coarse_w[...]
-    stacked[:, pl.ds(0, width)] = cot_ref[...]
-    for v in range(var_count):
-        stacked[:, pl.ds((v + 1) * width, width)] = inc_ref[v]
 
     @pl.when(lat == 0)
     def _():
@@ -306,6 +332,9 @@
     @pl.when(lat == planes - 1)
     def _():
         down_in[...] = jnp.zeros_like(down_in)
+
+    loads[0].wait()
+    loads[1].wait()
 
     pl.semaphore_wait(barrier, lon_count + planes - 2)
     table_start(0)
@@ -313,6 +342,9 @@
         for k in range(1, planes):
             for kind in kinds:
                 meta_copy(kind, lax.rem(lat + k, planes), lat).start()
+
+    for load in loads[2:]:
+        load.wait()
 
     @pl.loop(0, planes)
     def _(block):
@@ -321,11 +353,18 @@
         moved = dot(table, stacked[...]).astype(jnp.bfloat16)
         cot_out[block] = moved[:, :width].reshape(lon_count, segment, width)
         fields_out[block] = moved[:, width:].reshape(lon_count, segment, flat_width)
-        start_block(0, cot_out, cot_in, block)
+
+        @pl.when(block < half)
+        def _():
+            start_block(0, cot_out, cot_in, block)
 
     table_relay(0)
     start_block(1, fields_out, fields_in, 0)
     table_start(1)
+
+    @pl.loop(half, planes)
+    def _(block):
+        start_block(0, cot_out, cot_in, block)
 
     wait_meta((0, 1))
 
@@ -335,13 +374,16 @@
         first, second = column_of(back_in[block, 0:1, :]), column_of(back_in[block, 1:2, :])
         btab[block] = blend(first == spot, second == spot, column_of(back_share[block]))
 
-    @pl.loop(0, planes)
-    def _(block):
+    def column_sums(block):
         wait_block(0, cot_in, block)
         partial = dot(jnp.transpose(cot_in[block].reshape(part, width)), btab[block])
         for step in range(row_blocks):
             own[0, block * row_blocks + step] = partial[:, step * BLOCK : (step + 1) * BLOCK].astype(own.dtype)
             chain_begin(0, block * row_blocks + step)
+
+    @pl.loop(0, half)
+    def _(block):
+        column_sums(block)
 
     def build(group):
         depth = lw_ref.shape[2]
@@ -385,7 +427,6 @@
         coarse = interpolate(0, rows)
         kept[step] = coarse
         own[1, step] = bands(0, lw_count, 0, rows, coarse, jnp.zeros((width, BLOCK), jnp.float32)).astype(own.dtype)
-        chain_early(0, step)
 
     table_relay(1)
 
@@ -395,45 +436,43 @@
 
     @pl.loop(0, row_blocks)
     def _(step):
-        chain_early(0, step + row_blocks)
-        chain_late(0, step)
+        chain_early(0, step)
+
+    @pl.loop(half, planes)
+    def _(block):
+        column_sums(block)
 
     table_finish(1)
     table_wait(1)
 
     build(1)
 
-    @pl.loop(0, planes)
-    def _(turn):
-        def follow(unit):
-            chain_begin(1, unit)
-            chain_early(0, unit + 2 * row_blocks)
-            chain_late(0, unit + row_blocks)
-            chain_early(1, unit - 2 * row_blocks)
-            chain_late(1, unit - 3 * row_blocks)
-
-        @pl.when(turn == 0)
-        def _():
-            @pl.loop(0, row_blocks)
-            def _(step):
-                begun = own[1, step].astype(jnp.float32)
-                total = bands(lw_count, band_count, 0, sub_rows(step), kept[step], begun)
-                own[1, step] = total.astype(own.dtype)
-                follow(step)
-
-        @pl.when(turn > 0)
-        def _():
-            block = turn
-            gather_fields(block)
-
-            @pl.loop(0, row_blocks)
-            def _(step):
-                unit = block * row_blocks + step
-                rows = sub_rows(step)
-                coarse = interpolate(block, rows)
-                zero = jnp.zeros((width, BLOCK), jnp.float32)
-                own[1, unit] = bands(0, band_count, block, rows, coarse, zero).astype(own.dtype)
-                follow(unit)
+    def follow(unit):
+        chain_begin(1, unit)
+        chain_early(0, unit + row_blocks)
+        chain_late(0, unit)
+        chain_early(1, unit - 3 * row_blocks)
+        chain_late(1, unit - 4 * row_blocks)
+
+    @pl.loop(0, row_blocks)
+    def _(step):
+        begun = own[1, step].astype(jnp.float32)
+        total = bands(lw_count, band_count, 0, sub_rows(step), kept[step], begun)
+        own[1, step] = total.astype(own.dtype)
+        follow(step)
+
+    @pl.loop(1, planes)
+    def _(block):
+        gather_fields(block)
+
+        @pl.loop(0, row_blocks)
+        def _(step):
+            unit = block * row_blocks + step
+            rows = sub_rows(step)
+            coarse = interpolate(block, rows)
+            zero = jnp.zeros((width, BLOCK), jnp.float32)
+            own[1, unit] = bands(0, band_count, block, rows, coarse, zero).astype(own.dtype)
+            follow(unit)
 
     def finish_heat(block):
         for step in range(row_blocks):
@@ -442,13 +481,13 @@
             heat[pl.ds(step * BLOCK, BLOCK), :] = jnp.transpose(chain_total(1, unit)).astype(jnp.bfloat16)
         moved = dot(btab[block], heat[...]).astype(jnp.bfloat16)
         tend_out[block] = moved.reshape(lon_count, segment, width)
-        start_block(3, tend_out, result_in.at[:, :, :, pl.ds(0, width)], block)
-
-    @pl.loop(0, planes + 1)
+        return_block(3, tend_out, block)
+
+    @pl.loop(0, planes + 2)
     def _(turn):
-        @pl.when(turn > 0)
-        def _():
-            finish_heat(turn - 1)
+        @pl.when(turn > 1)
+        def _():
+            finish_heat(turn - 2)
 
         @pl.when(turn < planes)
         def _():
@@ -465,12 +504,31 @@
                     [(scale[b : b + 1, :] * coarse).astype(jnp.bfloat16) for b in range(band_count)], axis=0
                 )
                 adj[:, rows] = dot(wide[...], lifted).astype(jnp.bfloat16)
-                chain_early(1, unit + units - 2 * row_blocks)
-                chain_late(1, unit + units - 3 * row_blocks)
+                early, late = unit + units - 3 * row_blocks, unit + units - 4 * row_blocks
+
+                @pl.when(block < 2)
+                def _():
+                    chain_early(1, early)
+
+                @pl.when(block < planes - 1)
+                def _():
+                    chain_late(1, late)
+
+                first = units - row_blocks + 2 * step
+
+                @pl.when((block == 2) & (step < row_blocks // 2))
+                def _():
+                    chain_early(1, first)
+                    chain_early(1, first + 1)
+
+                @pl.when((block == planes - 1) & (step < row_blocks // 2))
+                def _():
+                    chain_late(1, first)
+                    chain_late(1, first + 1)
 
             moved = lax.dot_general(ctab[block], adj[...], (((1,), (1,)), ((), ())), preferred_element_type=jnp.float32)
             grad_out[block] = moved.astype(jnp.bfloat16).reshape(lon_count, segment, flat_width)
-            start_block(2, grad_out, result_in.at[:, :, :, pl.ds(width, flat_width)], block)
+            return_block(2, grad_out, block)
 
     for group in range(4):
         table_sent(group)
@@ -484,25 +542,39 @@
     wait_sent(0, cot_out)
     wait_sent(1, fields_out)
 
-    @pl.loop(0, planes)
-    def _(block):
-        wait_block(2, result_in.at[:, :, :, pl.ds(width, flat_width)], block)
-        wait_block(3, result_in.at[:, :, :, pl.ds(0, width)], block)
+    for block in range(early):
+        wait_return(block)
+
+    for kind, source in ((2, grad_out), (3, tend_out)):
+        piece = source.at[:, 0]
+        pltpu.make_async_copy(piece, piece, keep_sem.at[kind - 2]).wait()
+
+    def put(step):
+        rows = pl.ds(pl.multiple_of(step * FINAL, FINAL), FINAL)
+        return pltpu.make_async_copy(staged.at[rows], restored.at[rows], put_sem)
+
+    @pl.loop(0, col_count // FINAL)
+    def _(step):
+        rows = pl.ds(pl.multiple_of(step * FINAL, FINAL), FINAL)
+        table = pick(perm_ref[:, pl.ds(0, early * part)] == row_iota(FINAL, early * part, step * FINAL))
+        values = early_in[...].reshape(early * part, width + flat_width)
+        staged[rows, :] = dot(table, values).astype(jnp.bfloat16)
+        put(step).start()
+
+    for block in range(early, planes):
+        wait_return(block)
+    pltpu.make_async_copy(staged, restored, put_sem).wait()
 
     wait_sent(2, grad_out)
     wait_sent(3, tend_out)
 
-    for kind, source, start in ((2, grad_out, width), (3, tend_out, 0)):
-        piece = source.at[:, 0]
-        kept_piece = result_in.at[:, 0, :, pl.ds(start, source.shape[-1])]
-        pltpu.make_async_copy(piece, kept_piece, keep_sem.at[kind - 2]).wait()
-
-
-def restore_kernel(perm_ref, result_ref, tend_done, grad_done):
+
+def restore_kernel(perm_ref, result_ref, restored_ref, tend_done, grad_done):
     rows, width = tend_done.shape
-    col_count = result_ref.shape[0]
-    table = pick(perm_ref[...] == row_iota(rows, col_count, pl.program_id(0) * rows))
-    moved = dot(table, result_ref[...]).astype(jnp.bfloat16)
+    late = result_ref.shape[0]
+    slots = perm_ref[:, perm_ref.shape[1] - late :]
+    table = pick(slots == row_iota(rows, late, pl.program_id(0) * rows))
+    moved = (restored_ref[...].astype(jnp.float32) + dot(table, result_ref[...])).astype(jnp.bfloat16)
     tend_done[...] = moved[:, :width]
     for v in range(grad_done.shape[0]):
         grad_done[v] = moved[:, (v + 1) * width : (v + 2) * width]
@@ -535,8 +607,12 @@
     scale_rows = -(-(bands + 1) // 8) * 8
     wire = (2, planes * (row_count // BLOCK), width, BLOCK)
     half, full, whole = jnp.bfloat16, jnp.float32, jnp.int32
-    vmem = pl.BlockSpec(memory_space=pltpu.VMEM)
+    vmem, hbm = pl.BlockSpec(memory_space=pltpu.VMEM), pl.BlockSpec(memory_space=pl.ANY)
+    early = planes // 2
+    stack_width = (var_count + 1) * width
     scratch = [
+        ((early, lon_count, segment, stack_width), half),
+        ((col_count, stack_width), half),
         ((col_count, (var_count + 1) * width), half),
         (thin, half),
         (thin, half),
@@ -575,8 +651,8 @@
         (4,),
         (4, lon_count),
         (2,),
+        (3 + var_count,),
     )
-    stack_width = (var_count + 1) * width
     args = (
         owner_perm,
         jnp.transpose(increments, (1, 0, 2)),
@@ -591,13 +667,17 @@
         coarse_index,
         coarse_weight[None, :],
     )
-    received = pl.pallas_call(
+    result, restored = pl.pallas_call(
         radiate_kernel,
-        out_shape=jax.ShapeDtypeStruct((planes, lon_count, segment, stack_width), half),
-        in_specs=[vmem] * len(args),
-        out_specs=pl.BlockSpec(memory_space=pl.ANY),
+        out_shape=[
+            jax.ShapeDtypeStruct((planes - early, lon_count, segment, stack_width), half),
+            jax.ShapeDtypeStruct((col_count, stack_width), half),
+        ],
+        in_specs=[hbm if i in LOADED else vmem for i in range(len(args))],
+        out_specs=[hbm, hbm],
         scratch_shapes=[pltpu.VMEM(shape, kind) for shape, kind in scratch]
-        + [pltpu.SemaphoreType.DMA(shape) for shape in sems],
+        + [pltpu.SemaphoreType.DMA(shape) for shape in sems]
+        + [pltpu.SemaphoreType.DMA],
         compiler_params=pltpu.CompilerParams(
             vmem_limit_bytes=62 * 1024 * 1024, has_side_effects=True, collective_id=0
         ),
@@ -605,7 +685,9 @@
             flops=12 * planes * row_count * bands * flat_width * width, bytes_accessed=4 << 20, transcendentals=0
         ),
     )(*args)
-    steps = col_count // FINAL
+    rows = 2 * FINAL
+    steps = col_count // rows
+    late = (planes - early) * part
     tendency, gradient = pl.pallas_call(
         restore_kernel,
         grid=(steps,),
@@ -615,17 +697,18 @@
         ],
         in_specs=[
             pl.BlockSpec((1, col_count), lambda i: (0, 0)),
-            pl.BlockSpec((col_count, stack_width), lambda i: (0, 0)),
+            pl.BlockSpec((late, stack_width), lambda i: (0, 0)),
+            pl.BlockSpec((rows, stack_width), lambda i: (i, 0)),
         ],
         out_specs=[
-            pl.BlockSpec((FINAL, width), lambda i: (i, 0)),
-            pl.BlockSpec((var_count, FINAL, width), lambda i: (0, i, 0)),
+            pl.BlockSpec((rows, width), lambda i: (i, 0)),
+            pl.BlockSpec((var_count, rows, width), lambda i: (0, i, 0)),
         ],
-        compiler_params=pltpu.CompilerParams(vmem_limit_bytes=32 * 1024 * 1024),
+        compiler_params=pltpu.CompilerParams(vmem_limit_bytes=62 * 1024 * 1024),
         cost_estimate=pl.CostEstimate(
-            flops=2 * col_count * col_count * stack_width, bytes_accessed=4 << 20, transcendentals=0
+            flops=2 * col_count * late * stack_width, bytes_accessed=4 << 20, transcendentals=0
         ),
-    )(owner_perm, received.reshape(col_count, stack_width))
+    )(owner_perm, result.reshape(late, stack_width), restored)
     return (tendency, jnp.transpose(gradient, (1, 0, 2)))
 
 

time: 97.2 us -> 92.1 us (0.948)
  Pallas kernels: 94.8 us -> 91.2 us
  local copies, waits for them, and re-layouts: 1.59 us -> 0 us
    pallas_call x1, Pallas kernels: 88.9 us -> 86.2 us  [local(): pl.pallas_call(radiate_kernel, out_shape=[jax.ShapeDtypeStruct((planes -...]
    unnamed x4 -> x0, local copies, waits for them, and re-layouts: 1.59 us -> none
where the time goes in v4:
time: 92.1 us; the launch traced here: 91.9 us
  Pallas kernels  91.2 us (99%)
    pallas_call x1, Pallas kernels, local(): pl.pallas_call(radiate_kernel, out_shape=[jax.ShapeDtypeStruct((planes -...  86.2 us
    pallas_call x1, Pallas kernels, local(): pl.pallas_call(restore_kernel, grid=(steps,), out_shape=[jax.ShapeDtypeSt...  5.07 us

profile of v4, /device:TPU:0, one launch (start us, length us, event | category | flops | bytes accessed | tf_op | source)
XLA Modules:
  0.0 91.9 jit_solution(5429406346504411064)
XLA Ops:
  0.6 86.2 %shard_map.131 = (bf16[2,8,64,512]{3,2,1,0:T(8,128)(2,1)}, bf16[2048,512]{1,0:T(8,128)(2,1)}) custom-call(s32[1,2048]{1,0:T(1,128)} %perm_ref.3, bf16[3,2048,128]{2,1,0:T(8,128)(2,1)} %bitcast.6, bf16[2048,128]{1,0:T(8,128)(2,1)} %cot_ref.1, s32[2,2048]{1,0:T(2,128)} %back_ref.1, f32[1,2048]{1,0:T(1,128)} %bitcast.7, f32[16,1024]{1,0:T(8,128)} %lw_scale.1, ...), custom_call_target="tpu_custom_call" | custom-call | flops 72477573120 | bytes 4194304 | tf_op jit(solution)/shard_map/pallas_call | solution.py:670
  86.8 5.1 %shard_map.132 = (bf16[2048,128]{1,0:T(8,128)(2,1)}, bf16[3,2048,128]{2,1,0:T(8,128)(2,1)}) custom-call(s32[1,2048]{1,0:T(1,128)} %perm_ref.3, bf16[1024,512]{1,0:T(8,128)(2,1)} %bitcast.11, bf16[2048,512]{1,0:T(8,128)(2,1)} %get-tuple-element.7.restored_ref), custom_call_target="tpu_custom_call" | custom-call | flops 2147483648 | bytes 4194304 | tf_op jit(solution)/shard_map/pallas_call | solution.py:691

commit v5 on v4

--- a/solution.py
+++ b/solution.py
@@ -483,11 +483,13 @@
         tend_out[block] = moved.reshape(lon_count, segment, width)
         return_block(3, tend_out, block)
 
+    delay = jnp.where((lat == 0) | (lat == planes - 1), 2, 1)
+
     @pl.loop(0, planes + 2)
     def _(turn):
-        @pl.when(turn > 1)
-        def _():
-            finish_heat(turn - 2)
+        @pl.when((turn >= delay) & (turn < planes + delay))
+        def _():
+            finish_heat(turn - delay)
 
         @pl.when(turn < planes)
         def _():
@@ -510,7 +512,7 @@
                 def _():
                     chain_early(1, early)
 
-                @pl.when(block < planes - 1)
+                @pl.when(block < 3)
                 def _():
                     chain_late(1, late)
 
@@ -521,7 +523,7 @@
                     chain_early(1, first)
                     chain_early(1, first + 1)
 
-                @pl.when((block == planes - 1) & (step < row_blocks // 2))
+                @pl.when((block == 3) & (step < row_blocks // 2))
                 def _():
                     chain_late(1, first)
                     chain_late(1, first + 1)

time: 92.1 us -> 92.2 us (level)
  no operation moved by 1% of the time
where the time goes in v5:
time: 92.2 us; the launch traced here: 92 us
  Pallas kernels  91.3 us (99%)
    pallas_call x1, Pallas kernels, local(): pl.pallas_call(radiate_kernel, out_shape=[jax.ShapeDtypeStruct((planes -...  86.3 us
    pallas_call x1, Pallas kernels, local(): pl.pallas_call(restore_kernel, grid=(steps,), out_shape=[jax.ShapeDtypeSt...  5.07 us

profile of v5, /device:TPU:0, one launch (start us, length us, event | category | flops | bytes accessed | tf_op | source)
XLA Modules:
  0.0 92.0 jit_solution(15981452500893138671)
XLA Ops:
  0.6 86.3 %shard_map.131 = (bf16[2,8,64,512]{3,2,1,0:T(8,128)(2,1)}, bf16[2048,512]{1,0:T(8,128)(2,1)}) custom-call(s32[1,2048]{1,0:T(1,128)} %perm_ref.3, bf16[3,2048,128]{2,1,0:T(8,128)(2,1)} %bitcast.6, bf16[2048,128]{1,0:T(8,128)(2,1)} %cot_ref.1, s32[2,2048]{1,0:T(2,128)} %back_ref.1, f32[1,2048]{1,0:T(1,128)} %bitcast.7, f32[16,1024]{1,0:T(8,128)} %lw_scale.1, ...), custom_call_target="tpu_custom_call" | custom-call | flops 72477573120 | bytes 4194304 | tf_op jit(solution)/shard_map/pallas_call | solution.py:672
  86.9 5.1 %shard_map.132 = (bf16[2048,128]{1,0:T(8,128)(2,1)}, bf16[3,2048,128]{2,1,0:T(8,128)(2,1)}) custom-call(s32[1,2048]{1,0:T(1,128)} %perm_ref.3, bf16[1024,512]{1,0:T(8,128)(2,1)} %bitcast.11, bf16[2048,512]{1,0:T(8,128)(2,1)} %get-tuple-element.7.restored_ref), custom_call_target="tpu_custom_call" | custom-call | flops 2147483648 | bytes 4194304 | tf_op jit(solution)/shard_map/pallas_call | solution.py:693
